TPU v7x, 128 devices: a whole 4x4x4 slice. The times are simulated.
128 devices in a mesh: gx: 16 (over y_lo, x, core), gy: 8 (over z, y_hi).
Axes of the slice: x: 4, y: 4 (y_hi: 2, y_lo: 2; y = y_hi * 2 + y_lo), z: 4, core: 2. Of those that a mesh axis runs over, the one named last changes fastest.
Arguments:
- features: bfloat16 [65536, 128], P(('gx', 'gy')), may hold values from -6 to 6
- cache_in: bfloat16 [65536, 128], replicated, may hold values from -26 to 26
- cache_hidden: bfloat16 [65536, 128], replicated, may hold values from -26 to 26
- tiles: bfloat16 [128, 128, 256, 256], P(('gx', 'gy')), may hold values from -0.03125 to 0.03125
- tile_pos: int32 [128, 128, 2], P(('gx', 'gy')), may hold values from 0 to 1
- order: int32 [2, 128], replicated, may hold values from 0 to 127, each once within a row
- skip: int32 [2, 128], replicated, may hold values 0 or 1
- w_first: bfloat16 [128, 128], replicated, may hold values from -0.5 to 0.5
- w_second: bfloat16 [128, 128], replicated, may hold values from -0.5 to 0.5
Outputs:
- output: bfloat16 [65536, 128], P(('gx', 'gy'))
- drift: float32 [2], replicated
Inputs may be any that keep to these rules, and one draw needn't show every extreme that they name: `order`: each row names every block once.
All inputs are finite; a program needn't handle non-finite values.
Results may differ from a plain program's by a relative error of at most 0.0052.
Values may be sent and summed in bfloat16 or wider, within the bound.
No kernel may reach another device: no remote copies, remote signals or barrier semaphores. Data moves between devices by JAX's collectives and lax.ppermute only.
A program may use at most 192 MiB of HBM per device.

v0:
```python
import jax
import jax.numpy as jnp
from jax import lax
from jax.experimental import pallas as pl
from jax.experimental.pallas import tpu as pltpu
from jax.sharding import Mesh
from jax.sharding import PartitionSpec as P


AXES = ("ylo", "x", "core", "z", "yhi")
NB = 128
ROWS = 512
TS = 256
W = 128
DEPTH = 8
UNROLL = 4
MID = 8
LATE = 4
AX = ((1, 2, 0), (2, 0, 1))


def coords(i):
    return [(i // 16) % 4, (i % 2) * 2 + i // 64, (i // 2) % 4, (i // 8) % 2]


def block_id(x, y, z, core):
    return (y % 2) * 64 + x * 16 + core * 8 + z * 2 + y // 2


def stage_perm(stage, shift):
    pairs = []
    for i in range(NB):
        c = coords(i)
        a = AX[c[3]][stage]
        c[a] = (c[a] + shift) % 4
        pairs.append((i, block_id(*c)))
    return pairs


PERM = {(s, k): stage_perm(s, k) for s in range(3) for k in (1, 2, 3)}
SWAP = [(i, i ^ 8) for i in range(NB)]


def shift(value, stage, k):
    return lax.ppermute(value, AXES, PERM[(stage, k)])


def swap(value):
    return lax.ppermute(value, AXES, SWAP)


def gather(block):
    s1 = block[None]
    s4 = jnp.concatenate([s1] + [shift(s1, 0, k) for k in (1, 2, 3)], 0)
    s16 = jnp.concatenate([s4] + [shift(s4, 1, k) for k in (1, 2, 3)], 0)
    lo, hi = s16[:8], s16[8:]
    a1 = shift(lo, 2, 1)
    b3 = shift(hi, 2, 3)
    b1 = shift(hi, 2, 1)
    a3 = shift(lo, 2, 3)
    f1 = shift(a1, 2, 1)
    f3 = shift(b3, 2, 3)
    near = [s16, swap(s16)]
    mid = [a1, b3, b1, a3]
    mid += [swap(p) for p in mid]
    late = [f1, f3]
    late += [swap(p) for p in late]
    return near, mid, late


def item_blocks():
    k1, k2, k3, other = [], [], [], []

    def add(slots, third, o):
        for s in slots:
            k1.append(s % 4)
            k2.append(s // 4)
            k3.append(third)
            other.append(o)

    for o in (0, 1):
        add(range(16), 0, o)
    for group in (((0, 1), (8, 3), (8, 1), (0, 3)), ((0, 2), (8, 2))):
        for o in (0, 1):
            for slots, third in group:
                add(range(slots, slots + 8), third, o)
    k1, k2, k3, other = (jnp.array(v, jnp.int32) for v in (k1, k2, k3, other))
    x = lax.axis_index("x")
    y = lax.axis_index("yhi") * 2 + lax.axis_index("ylo")
    z = lax.axis_index("z")
    core = lax.axis_index("core") ^ other
    zero = core == 0
    bx = (x - jnp.where(zero, k3, k2)) & 3
    by = (y - jnp.where(zero, k1, k3)) & 3
    bz = (z - jnp.where(zero, k2, k1)) & 3
    return (by & 1) * 64 + bx * 16 + core * 8 + bz * 2 + (by >> 1)


def groups_of(n):
    return (n + (UNROLL - 1)) // UNROLL


def pad(ref, n):
    for u in range(UNROLL - 1):
        ref[n + u] = 2


def tile_copy(tiles, tbuf, tsem, code, slot):
    return pltpu.make_async_copy(tiles.at[(code >> 4) & 127], tbuf.at[slot], tsem.at[slot])


def run(n, start, wait, source, codes, accs, tbuf):
    total = groups_of(n) * UNROLL
    for d in range(DEPTH):
        @pl.when(d < total)
        def _(d=d):
            start(d, d)

    def body(g, c):
        first = g * UNROLL
        slot0 = (g & (DEPTH // UNROLL - 1)) * UNROLL
        for u in range(UNROLL):
            wait(first + u, slot0 + u)
        for u in range(UNROLL):
            up = (codes[first + u] & 3) * TS
            accs[u, pl.ds(up, TS), :] += jnp.dot(
                tbuf[slot0 + u],
                source(first + u, slot0 + u),
                preferred_element_type=jnp.float32,
            )
        for u in range(UNROLL):
            @pl.when(first + u + DEPTH < total)
            def _(u=u):
                start(first + u + DEPTH, slot0 + u)
        return c

    lax.fori_loop(0, groups_of(n), body, 0)


def run_staged(n, codes, accs, tiles, tbuf, tsem, stage):
    run(
        n,
        lambda t, slot: tile_copy(tiles, tbuf, tsem, codes[t], slot).start(),
        lambda t, slot: tile_copy(tiles, tbuf, tsem, codes[t], slot).wait(),
        lambda t, slot: stage[t],
        codes,
        accs,
        tbuf,
    )


def fill_stage(codes, first, last, ref, stage):
    def body(t, c):
        code = codes[t]
        stage[t] = ref[code >> 16, pl.ds(((code >> 2) & 1) * TS, TS), :]
        return c

    lax.fori_loop(first, last, body, 0)


def total_of(accs):
    total = accs[0, 0:ROWS, :]
    for u in range(1, UNROLL):
        total = total + accs[u, 0:ROWS, :]
    return total


def early_kernel(
    order, skip, pos, jtab, own, tiles, cached, s16, p16, block,
    acc, mlist, moff, llist, loff, drift,
    clist, slist, flags, accs, tbuf, sbuf, stage, own_buf, tsem, ssem, osem,
):
    me = own[0]
    own_copy = pltpu.make_async_copy(cached.at[me], own_buf, osem)
    own_copy.start()

    def set_flag(r, c):
        flags[order[r]] = 1 - skip[r]
        return c

    lax.fori_loop(0, NB, set_flag, 0)
    flags[me] = 1

    def split(first, last, nc, nl, slots, fresh_list):
        def build(t, c):
            nc, nl = c
            j = jtab[t]
            fresh = flags[j]
            code = ((t & (slots - 1)) << 16) | (j << 4) | (pos[2 * j + 1] << 2) | pos[2 * j]
            clist[nc] = code
            fresh_list[nl] = code
            return nc + 1 - fresh, nl + fresh

        return lax.fori_loop(first, last, build, (nc, nl))

    nc, n_own = split(0, 16, 0, 0, 16, slist)
    nc, n_near = split(16, 32, nc, n_own, 16, slist)
    base = 32
    for pieces, fresh_list, off in ((MID, mlist, moff), (LATE, llist, loff)):
        nl = 0
        for p in range(pieces):
            off[p] = nl
            nc, nl = split(base, base + 8, nc, nl, 8, fresh_list)
            base += 8
        off[pieces] = nl
        pad(fresh_list, nl)
    pad(clist, nc)
    pad(slist, n_near)
    accs[...] = jnp.zeros_like(accs)

    def source_copy(t, slot):
        code = clist[t]
        return pltpu.make_async_copy(
            cached.at[(code >> 4) & 127, pl.ds(((code >> 2) & 1) * TS, TS), :],
            sbuf.at[slot],
            ssem.at[slot],
        )

    def start(t, slot):
        tile_copy(tiles, tbuf, tsem, clist[t], slot).start()
        source_copy(t, slot).start()

    def wait(t, slot):
        tile_copy(tiles, tbuf, tsem, clist[t], slot).wait()
        source_copy(t, slot).wait()

    run(nc, start, wait, lambda t, slot: sbuf[slot], clist, accs, tbuf)
    fill_stage(slist, 0, n_own, s16, stage)
    fill_stage(slist, n_own, n_near, p16, stage)
    run_staged(n_near, slist, accs, tiles, tbuf, tsem, stage)
    acc[...] = total_of(accs)
    own_copy.wait()
    diff = block[0:ROWS, :].astype(jnp.float32) - own_buf[...].astype(jnp.float32)
    drift[...] = jnp.broadcast_to(jnp.sum(diff * diff, axis=0, keepdims=True), (8, W))


def add_pieces(codes, off, tiles, pieces, accs, tbuf, stage, tsem):
    accs[...] = jnp.zeros_like(accs)
    for p, ref in enumerate(pieces):
        fill_stage(codes, off[p], off[p + 1], ref, stage)
    run_staged(off[len(pieces)], codes, accs, tiles, tbuf, tsem, stage)
    return total_of(accs)


def mid_kernel(codes, off, acc_in, tiles, *rest):
    pieces = rest[:MID]
    acc, accs, tbuf, stage, tsem = rest[MID:]
    acc[...] = acc_in[...] + add_pieces(codes, off, tiles, pieces, accs, tbuf, stage, tsem)


def split3(row):
    hi = row.astype(jnp.bfloat16).astype(jnp.float32)
    mid = (row - hi).astype(jnp.bfloat16).astype(jnp.float32)
    return hi, mid, row - hi - mid


def late_first_kernel(
    codes, off, own, acc_in, drift_in, weight, tiles, cached, *rest
):
    pieces = rest[:LATE]
    payload, accs, tbuf, stage, own_buf, tsem, osem = rest[LATE:]
    own_copy = pltpu.make_async_copy(cached.at[own[0]], own_buf, osem)
    own_copy.start()
    total = acc_in[...] + add_pieces(codes, off, tiles, pieces, accs, tbuf, stage, tsem)
    hidden = jnp.maximum(
        jnp.dot(
            total.astype(jnp.bfloat16), weight[...], preferred_element_type=jnp.float32
        ),
        0.0,
    ).astype(jnp.bfloat16)
    payload[0:ROWS, :] = hidden
    own_copy.wait()
    diff = hidden.astype(jnp.float32) - own_buf[...].astype(jnp.float32)
    second = jnp.sum(diff * diff, axis=0, keepdims=True)
    row = lax.broadcasted_iota(jnp.int32, (16, W), 0)
    extra = jnp.zeros((16, W), jnp.float32)
    for k, part in enumerate(split3(drift_in[0:1, :]) + split3(second)):
        extra = jnp.where(row == k, jnp.broadcast_to(part, (16, W)), extra)
    payload[ROWS:, :] = extra.astype(jnp.bfloat16)


def late_second_kernel(codes, off, jtab, acc_in, weight, tiles, *rest):
    pieces = rest[: 2 + MID + LATE]
    output, drift, accs, tbuf, stage, ext, tsem = rest[2 + MID + LATE :]
    total = acc_in[...] + add_pieces(
        codes, off, tiles, pieces[2 + MID :], accs, tbuf, stage, tsem
    )
    output[...] = jnp.dot(
        total.astype(jnp.bfloat16), weight[...], preferred_element_type=jnp.float32
    ).astype(jnp.bfloat16)
    base = 0
    for ref in pieces:
        for s in range(ref.shape[0]):
            ext[jtab[base + s]] = ref[s, ROWS:, :]
        base += ref.shape[0]
    total = jnp.sum(ext[...].astype(jnp.float32), axis=0)
    cells = 1.0 / (NB * ROWS * W)
    drift[0] = jnp.sum(total[0:3, :]) * cells
    drift[1] = jnp.sum(total[3:6, :]) * cells


SMEM = pl.BlockSpec(memory_space=pltpu.SMEM)
VMEM = pl.BlockSpec(memory_space=pltpu.VMEM)
HBM = pl.BlockSpec(memory_space=pltpu.HBM)


ACCS = pltpu.VMEM((UNROLL, 3 * TS, W), jnp.float32)
TILE_RING = pltpu.VMEM((DEPTH, TS, TS), jnp.bfloat16)
RING_SEMS = pltpu.SemaphoreType.DMA((DEPTH,))
BLOCK = pltpu.VMEM((ROWS, W), jnp.bfloat16)


def stage_of(items):
    return pltpu.VMEM((items + UNROLL, TS, W), jnp.bfloat16)


def params(mib):
    return pltpu.CompilerParams(vmem_limit_bytes=mib * 1024 * 1024)


def cost(items):
    return pl.CostEstimate(
        flops=items * 2 * TS * TS * W, transcendentals=0, bytes_accessed=items * 196608
    )


def codes_shape(items):
    return jax.ShapeDtypeStruct((items + 16,), jnp.int32)


def early(order, skip, pos, jtab, own, tiles, cached, near, block):
    return pl.pallas_call(
        early_kernel,
        out_shape=(
            jax.ShapeDtypeStruct((ROWS, W), jnp.float32),
            codes_shape(8 * MID),
            jax.ShapeDtypeStruct((16,), jnp.int32),
            codes_shape(8 * LATE),
            jax.ShapeDtypeStruct((16,), jnp.int32),
            jax.ShapeDtypeStruct((8, W), jnp.float32),
        ),
        in_specs=[SMEM] * 5 + [HBM] * 2 + [VMEM] * 3,
        out_specs=(VMEM, SMEM, SMEM, SMEM, SMEM, VMEM),
        scratch_shapes=[
            pltpu.SMEM((NB + 8,), jnp.int32),
            pltpu.SMEM((64,), jnp.int32),
            pltpu.SMEM((NB,), jnp.int32),
            ACCS,
            TILE_RING,
            pltpu.VMEM((DEPTH, TS, W), jnp.bfloat16),
            stage_of(32),
            BLOCK,
            RING_SEMS,
            RING_SEMS,
            pltpu.SemaphoreType.DMA,
        ],
        compiler_params=params(16),
        cost_estimate=cost(80),
        name="early_sum",
    )(order, skip, pos, jtab, own, tiles, cached, *near, block)


def mid_sum(codes, off, acc, tiles, pieces):
    return pl.pallas_call(
        mid_kernel,
        out_shape=jax.ShapeDtypeStruct((ROWS, W), jnp.float32),
        in_specs=[SMEM] * 2 + [VMEM] + [HBM] + [VMEM] * MID,
        out_specs=VMEM,
        scratch_shapes=[ACCS, TILE_RING, stage_of(8 * MID), RING_SEMS],
        compiler_params=params(20),
        cost_estimate=cost(32),
        name="mid_sum",
    )(codes, off, acc, tiles, *pieces)


def late_first(codes, off, own, acc, drift, weight, tiles, cached, pieces):
    return pl.pallas_call(
        late_first_kernel,
        out_shape=jax.ShapeDtypeStruct((ROWS + 16, W), jnp.bfloat16),
        in_specs=[SMEM] * 3 + [VMEM] * 3 + [HBM] * 2 + [VMEM] * LATE,
        out_specs=VMEM,
        scratch_shapes=[
            ACCS,
            TILE_RING,
            stage_of(8 * LATE),
            BLOCK,
            RING_SEMS,
            pltpu.SemaphoreType.DMA,
        ],
        compiler_params=params(16),
        cost_estimate=cost(16),
        name="late_first",
    )(codes, off, own, acc, drift, weight, tiles, cached, *pieces)


def late_second(codes, off, jtab, acc, weight, tiles, pieces):
    return pl.pallas_call(
        late_second_kernel,
        out_shape=(
            jax.ShapeDtypeStruct((ROWS, W), jnp.bfloat16),
            jax.ShapeDtypeStruct((2,), jnp.float32),
        ),
        in_specs=[SMEM] * 3 + [VMEM] * 2 + [HBM] + [VMEM] * len(pieces),
        out_specs=(VMEM, SMEM),
        scratch_shapes=[
            ACCS,
            TILE_RING,
            stage_of(8 * LATE),
            pltpu.VMEM((NB, 16, W), jnp.bfloat16),
            RING_SEMS,
        ],
        compiler_params=params(20),
        cost_estimate=cost(16),
        name="late_second",
    )(codes, off, jtab, acc, weight, tiles, *pieces)


def in_hbm(value):
    return pltpu.with_memory_space_constraint(value, pltpu.HBM)


def on_device(features, cache_in, cache_hidden, tiles, tile_pos, order, skip, w_first, w_second):
    tiles = in_hbm(tiles[0])
    pos = tile_pos[0].reshape(2 * NB)
    own = lax.axis_index(AXES)[None].astype(jnp.int32)
    jtab = item_blocks()
    cache_in = in_hbm(cache_in.reshape(NB, ROWS, W))
    cache_hidden = in_hbm(cache_hidden.reshape(NB, ROWS, W))

    near, mid, late = gather(features)
    acc, mlist, moff, llist, loff, drift_in = early(
        order[0], skip[0], pos, jtab, own, tiles, cache_in, near, features
    )
    acc = mid_sum(mlist, moff, acc, tiles, mid)
    payload = late_first(
        llist, loff, own, acc, drift_in, w_first, tiles, cache_hidden, late
    )

    near, mid, late = gather(payload)
    acc, mlist, moff, llist, loff, _ = early(
        order[1], skip[1], pos, jtab, own, tiles, cache_hidden, near, payload
    )
    acc = mid_sum(mlist, moff, acc, tiles, mid)
    return late_second(llist, loff, jtab, acc, w_second, tiles, near + mid + late)


def solution(mesh):
    split = Mesh(mesh.devices.reshape(2, 4, 2, 4, 2), AXES)
    both = AXES
    in_specs = (
        P(both, None),
        P(),
        P(),
        P(both, None, None, None),
        P(both, None, None),
        P(),
        P(),
        P(),
        P(),
    )
    out_specs = (P(both, None), P())
    return jax.shard_map(
        on_device, mesh=split, in_specs=in_specs, out_specs=out_specs, check_vma=False
    )
```

profile of v0, /device:TPU:1, one launch (start us, length us, event | category | flops | bytes accessed | tf_op | source)
XLA Modules:
  0.0 219.8 jit_solution(7403790899913524847)
XLA Ops:
  0.6 2.5 %collective-permute-start = (bf16[1,512,128]{2,1,0:T(8,128)(2,1)}, bf16[1,512,128]{2,1,0:T(8,128)(2,1)S(1)}, u32[]{:S(2)}, u32[]{:S(2)}) collective-permute-start(bf16[1,512,128]{2,1,0:T(8,128)(2,1)} %bitcast.22), channel_id=1, source_target_pairs={{0,64},{1,65},{2,66},{3,67},{4,68},{5,69},{6,70},{7,71},{8,10},{9,... | collective-permute-start | bytes 393224 | tf_op jit(solution)/shard_map/ppermute | solution.py:45
  3.2 3.3 %collective-permute-start.1 = (bf16[1,512,128]{2,1,0:T(8,128)(2,1)}, bf16[1,512,128]{2,1,0:T(8,128)(2,1)S(1)}, u32[]{:S(2)}, u32[]{:S(2)}) collective-permute-start(bf16[1,512,128]{2,1,0:T(8,128)(2,1)} %bitcast.23), channel_id=1, source_target_pairs={{0,1},{1,0},{2,3},{3,2},{4,5},{5,4},{6,7},{7,6},{8,12},{9,13},{10,... | collective-permute-start | bytes 393224 | tf_op jit(solution)/shard_map/ppermute | solution.py:45
  8.1 2.6 %collective-permute-done.1 = bf16[1,512,128]{2,1,0:T(8,128)(2,1)S(1)} collective-permute-done((bf16[1,512,128]{2,1,0:T(8,128)(2,1)}, bf16[1,512,128]{2,1,0:T(8,128)(2,1)S(1)}, u32[]{:S(2)}, u32[]{:S(2)}) %collective-permute-start.1) | collective-permute-done | bytes 131104 | tf_op jit(solution)/shard_map/ppermute | solution.py:45
  13.0 2.5 %collective-permute-start.4 = (bf16[4,512,128]{2,1,0:T(8,128)(2,1)S(1)}, bf16[4,512,128]{2,1,0:T(8,128)(2,1)S(1)}, u32[]{:S(2)}, u32[]{:S(2)}) collective-permute-start(bf16[4,512,128]{2,1,0:T(8,128)(2,1)S(1)} %pad_maximum_fusion.1), channel_id=1, source_target_pairs={{0,4},{1,5},{2,6},{3,7},{4,0},{5,1},{6,2},{7,3},{8,40},{9,41},{10,... | collective-permute-start | bytes 1572872 | tf_op jit(solution)/shard_map/ppermute | solution.py:45
  17.8 3.6 %collective-permute-done.3 = bf16[4,512,128]{2,1,0:T(8,128)(2,1)S(1)} collective-permute-done((bf16[4,512,128]{2,1,0:T(8,128)(2,1)S(1)}, bf16[4,512,128]{2,1,0:T(8,128)(2,1)S(1)}, u32[]{:S(2)}, u32[]{:S(2)}) %collective-permute-start.3) | collective-permute-done | bytes 524320 | tf_op jit(solution)/shard_map/ppermute | solution.py:45
  21.6 6.3 %collective-permute-done.4 = bf16[4,512,128]{2,1,0:T(8,128)(2,1)S(1)} collective-permute-done((bf16[4,512,128]{2,1,0:T(8,128)(2,1)S(1)}, bf16[4,512,128]{2,1,0:T(8,128)(2,1)S(1)}, u32[]{:S(2)}, u32[]{:S(2)}) %collective-permute-start.4) | collective-permute-done | bytes 524320 | tf_op jit(solution)/shard_map/ppermute | solution.py:45
  28.4 3.3 %collective-permute-start.6 = (bf16[16,512,128]{2,1,0:T(8,128)(2,1)S(1)}, bf16[16,512,128]{2,1,0:T(8,128)(2,1)S(1)}, u32[]{:S(2)}, u32[]{:S(2)}) collective-permute-start(bf16[16,512,128]{2,1,0:T(8,128)(2,1)S(1)} %get-tuple-element.31.s16), channel_id=1, source_target_pairs={{0,8},{1,9},{2,10},{3,11},{4,12},{5,13},{6,14},{7,15},{8,0},{9,1},... | collective-permute-start | bytes 6291464 | tf_op jit(solution)/shard_map/ppermute | solution.py:49
  31.6 2.3 %collective-permute-start.8 = (bf16[8,512,128]{2,1,0:T(8,128)(2,1)S(1)}, bf16[8,512,128]{2,1,0:T(8,128)(2,1)S(1)}, u32[]{:S(2)}, u32[]{:S(2)}) collective-permute-start(bf16[8,512,128]{2,1,0:T(8,128)(2,1)S(1)} %get-tuple-element.30), channel_id=1, source_target_pairs={{0,48},{1,49},{2,50},{3,51},{4,52},{5,53},{6,54},{7,55},{8,73},{9,... | collective-permute-start | bytes 3145736 | tf_op jit(solution)/shard_map/ppermute | solution.py:45
  33.9 2.7 %collective-permute-start.10 = (bf16[8,512,128]{2,1,0:T(8,128)(2,1)S(1)}, bf16[8,512,128]{2,1,0:T(8,128)(2,1)}, u32[]{:S(2)}, u32[]{:S(2)}) collective-permute-start(bf16[8,512,128]{2,1,0:T(8,128)(2,1)S(1)} %get-tuple-element.34), channel_id=1, source_target_pairs={{0,48},{1,49},{2,50},{3,51},{4,52},{5,53},{6,54},{7,55},{8,73},{9,... | collective-permute-start | bytes 3145736 | tf_op jit(solution)/shard_map/ppermute | solution.py:45
  36.6 9.1 %collective-permute-done.8.rest_1_ = bf16[8,512,128]{2,1,0:T(8,128)(2,1)S(1)} collective-permute-done((bf16[8,512,128]{2,1,0:T(8,128)(2,1)S(1)}, bf16[8,512,128]{2,1,0:T(8,128)(2,1)S(1)}, u32[]{:S(2)}, u32[]{:S(2)}) %collective-permute-start.8) | collective-permute-done | bytes 1048608 | tf_op jit(solution)/shard_map/ppermute | solution.py:45
  46.8 2.4 %collective-permute-done.9.rest_2_ = bf16[8,512,128]{2,1,0:T(8,128)(2,1)} collective-permute-done((bf16[8,512,128]{2,1,0:T(8,128)(2,1)S(1)}, bf16[8,512,128]{2,1,0:T(8,128)(2,1)}, u32[]{:S(2)}, u32[]{:S(2)}) %collective-permute-start.9) | collective-permute-done | bytes 1048608 | tf_op jit(solution)/shard_map/ppermute | solution.py:45
  49.2 11.2 %collective-permute-done.7.rest_0_ = bf16[8,512,128]{2,1,0:T(8,128)(2,1)} collective-permute-done((bf16[8,512,128]{2,1,0:T(8,128)(2,1)S(1)}, bf16[8,512,128]{2,1,0:T(8,128)(2,1)}, u32[]{:S(2)}, u32[]{:S(2)}) %collective-permute-start.7) | collective-permute-done | bytes 1048608 | tf_op jit(solution)/shard_map/ppermute | solution.py:45
  64.7 3.5 %collective-permute-done.16.rest_1_ = bf16[8,512,128]{2,1,0:T(8,128)(2,1)} collective-permute-done((bf16[8,512,128]{2,1,0:T(8,128)(2,1)S(1)}, bf16[8,512,128]{2,1,0:T(8,128)(2,1)}, u32[]{:S(2)}, u32[]{:S(2)}) %collective-permute-start.16) | collective-permute-done | bytes 1048608 | tf_op jit(solution)/shard_map/ppermute | solution.py:45
  69.3 6.6 %collective-permute-done.15.rest_0_ = bf16[8,512,128]{2,1,0:T(8,128)(2,1)} collective-permute-done((bf16[8,512,128]{2,1,0:T(8,128)(2,1)}, bf16[8,512,128]{2,1,0:T(8,128)(2,1)}, u32[]{:S(2)}, u32[]{:S(2)}) %collective-permute-start.15) | collective-permute-done | bytes 1048608 | tf_op jit(solution)/shard_map/ppermute | solution.py:45
  75.9 2.3 %collective-permute-start.17 = (bf16[8,512,128]{2,1,0:T(8,128)(2,1)}, bf16[8,512,128]{2,1,0:T(8,128)(2,1)}, u32[]{:S(2)}, u32[]{:S(2)}) collective-permute-start(bf16[8,512,128]{2,1,0:T(8,128)(2,1)} %collective-permute-done.15.rest_0_), channel_id=1, source_target_pairs={{0,8},{1,9},{2,10},{3,11},{4,12},{5,13},{6,14},{7,15},{8,0},{9,1},... | collective-permute-start | bytes 3145736 | tf_op jit(solution)/shard_map/ppermute | solution.py:49
  80.1 19.5 %early_sum.2 = (f32[512,128]{1,0:T(8,128)S(1)}, s32[80]{0:T(128)S(1)}, s32[16]{0:T(128)S(1)}, s32[48]{0:T(128)S(1)}, s32[16]{0:T(128)S(1)}, /*index=5*/f32[8,128]{1,0:T(8,128)S(1)}) custom-call(s32[128]{0:T(128)S(1)} %get-tuple-element.57.order, s32[128]{0:T(128)S(1)} %get-tuple-element.52.skip, s32[256]{0:T(256)S(1)} %reshape_squeeze.3.pos, ...), custom_call_target="tpu_custom_call" | custom-call | flops 1342177280 | bytes 15728640 | tf_op jit(solution)/shard_map/early_sum/pallas_call | solution.py:332
  99.7 8.8 %mid_sum.2.acc_in = f32[512,128]{1,0:T(8,128)S(1)} custom-call(s32[80]{0:T(128)S(1)} %get-tuple-element.15.codes, s32[16]{0:T(128)S(1)} %get-tuple-element.16.off, f32[512,128]{1,0:T(8,128)S(1)} %get-tuple-element.17.acc_in, bf16[128,256,256]{2,1,0:T(8,128)(2,1)} %bitcast.27, bf16[8,512,128]{2,1,0:T(8,128)(2,1)} %collective-permute-done.7.rest_0_, ...), custom_call_target="tpu_custom_call" | custom-call | flops 536870912 | bytes 6291456 | tf_op jit(solution)/shard_map/mid_sum/pallas_call | solution.py:364
  108.6 7.0 %late_first.1.block = bf16[528,128]{1,0:T(8,128)(2,1)S(1)} custom-call(s32[48]{0:T(128)S(1)} %get-tuple-element.13.codes, s32[16]{0:T(128)S(1)} %get-tuple-element.14.off, s32[1]{0:T(128)} %bitcast.2.own, f32[512,128]{1,0:T(8,128)S(1)} %mid_sum.2.acc_in, f32[8,128]{1,0:T(8,128)S(1)} %get-tuple-element.18.drift_in, bf16[128,128]{1,0:T(8,128)(2,1)S(1)} %copy-done.6, ...), custom_call_target="tpu_custom_call" | custom-call | flops 268435456 | bytes 3145728 | tf_op jit(solution)/shard_map/late_first/pallas_call | solution.py:377
  115.6 2.5 %collective-permute-start.19 = (bf16[1,528,128]{2,1,0:T(8,128)(2,1)S(1)}, bf16[1,528,128]{2,1,0:T(8,128)(2,1)S(1)}, u32[]{:S(2)}, u32[]{:S(2)}) collective-permute-start(bf16[1,528,128]{2,1,0:T(8,128)(2,1)S(1)} %bitcast.18), channel_id=1, source_target_pairs={{0,64},{1,65},{2,66},{3,67},{4,68},{5,69},{6,70},{7,71},{8,10},{9,... | collective-permute-start | bytes 405512 | tf_op jit(solution)/shard_map/ppermute | solution.py:45
  121.0 2.7 %collective-permute-done.20 = bf16[1,528,128]{2,1,0:T(8,128)(2,1)S(1)} collective-permute-done((bf16[1,528,128]{2,1,0:T(8,128)(2,1)S(1)}, bf16[1,528,128]{2,1,0:T(8,128)(2,1)S(1)}, u32[]{:S(2)}, u32[]{:S(2)}) %collective-permute-start.20) | collective-permute-done | bytes 135200 | tf_op jit(solution)/shard_map/ppermute | solution.py:45
  127.0 12.4 %collective-permute-done.22 = bf16[4,528,128]{2,1,0:T(8,128)(2,1)S(1)} collective-permute-done((bf16[4,528,128]{2,1,0:T(8,128)(2,1)S(1)}, bf16[4,528,128]{2,1,0:T(8,128)(2,1)S(1)}, u32[]{:S(2)}, u32[]{:S(2)}) %collective-permute-start.22) | collective-permute-done | bytes 540704 | tf_op jit(solution)/shard_map/ppermute | solution.py:45
  140.2 2.6 %collective-permute-start.25 = (bf16[16,528,128]{2,1,0:T(8,128)(2,1)S(1)}, bf16[16,528,128]{2,1,0:T(8,128)(2,1)S(1)}, u32[]{:S(2)}, u32[]{:S(2)}) collective-permute-start(bf16[16,528,128]{2,1,0:T(8,128)(2,1)S(1)} %get-tuple-element.25.s16.rest_0_), channel_id=1, source_target_pairs={{0,8},{1,9},{2,10},{3,11},{4,12},{5,13},{6,14},{7,15},{8,0},{9,1},... | collective-permute-start | bytes 6488072 | tf_op jit(solution)/shard_map/ppermute | solution.py:49
  142.9 2.4 %collective-permute-start.27 = (bf16[8,528,128]{2,1,0:T(8,128)(2,1)S(1)}, bf16[8,528,128]{2,1,0:T(8,128)(2,1)S(1)}, u32[]{:S(2)}, u32[]{:S(2)}) collective-permute-start(bf16[8,528,128]{2,1,0:T(8,128)(2,1)S(1)} %get-tuple-element.24), channel_id=1, source_target_pairs={{0,48},{1,49},{2,50},{3,51},{4,52},{5,53},{6,54},{7,55},{8,73},{9,... | collective-permute-start | bytes 3244040 | tf_op jit(solution)/shard_map/ppermute | solution.py:45
  145.3 2.7 %collective-permute-start.29 = (bf16[8,528,128]{2,1,0:T(8,128)(2,1)S(1)}, bf16[8,528,128]{2,1,0:T(8,128)(2,1)S(1)}, u32[]{:S(2)}, u32[]{:S(2)}) collective-permute-start(bf16[8,528,128]{2,1,0:T(8,128)(2,1)S(1)} %get-tuple-element.28), channel_id=1, source_target_pairs={{0,48},{1,49},{2,50},{3,51},{4,52},{5,53},{6,54},{7,55},{8,73},{9,... | collective-permute-start | bytes 3244040 | tf_op jit(solution)/shard_map/ppermute | solution.py:45
  148.0 9.4 %collective-permute-done.27.rest_1_.rest_3_ = bf16[8,528,128]{2,1,0:T(8,128)(2,1)S(1)} collective-permute-done((bf16[8,528,128]{2,1,0:T(8,128)(2,1)S(1)}, bf16[8,528,128]{2,1,0:T(8,128)(2,1)S(1)}, u32[]{:S(2)}, u32[]{:S(2)}) %collective-permute-start.27) | collective-permute-done | bytes 1081376 | tf_op jit(solution)/shard_map/ppermute | solution.py:45
  158.1 2.7 %collective-permute-done.28.rest_2_.rest_4_ = bf16[8,528,128]{2,1,0:T(8,128)(2,1)S(1)} collective-permute-done((bf16[8,528,128]{2,1,0:T(8,128)(2,1)S(1)}, bf16[8,528,128]{2,1,0:T(8,128)(2,1)S(1)}, u32[]{:S(2)}, u32[]{:S(2)}) %collective-permute-start.28) | collective-permute-done | bytes 1081376 | tf_op jit(solution)/shard_map/ppermute | solution.py:45
  160.8 11.3 %collective-permute-done.26.rest_0_.rest_2_ = bf16[8,528,128]{2,1,0:T(8,128)(2,1)S(1)} collective-permute-done((bf16[8,528,128]{2,1,0:T(8,128)(2,1)S(1)}, bf16[8,528,128]{2,1,0:T(8,128)(2,1)S(1)}, u32[]{:S(2)}, u32[]{:S(2)}) %collective-permute-start.26) | collective-permute-done | bytes 1081376 | tf_op jit(solution)/shard_map/ppermute | solution.py:45
  172.7 7.8 %collective-permute-done.35.rest_11_ = bf16[8,528,128]{2,1,0:T(8,128)(2,1)S(1)} collective-permute-done((bf16[8,528,128]{2,1,0:T(8,128)(2,1)S(1)}, bf16[8,528,128]{2,1,0:T(8,128)(2,1)S(1)}, u32[]{:S(2)}, u32[]{:S(2)}) %collective-permute-start.35) | collective-permute-done | bytes 1081376 | tf_op jit(solution)/shard_map/ppermute | solution.py:45
  181.3 6.0 %collective-permute-done.34.rest_10_ = bf16[8,528,128]{2,1,0:T(8,128)(2,1)S(1)} collective-permute-done((bf16[8,528,128]{2,1,0:T(8,128)(2,1)S(1)}, bf16[8,528,128]{2,1,0:T(8,128)(2,1)S(1)}, u32[]{:S(2)}, u32[]{:S(2)}) %collective-permute-start.34) | collective-permute-done | bytes 1081376 | tf_op jit(solution)/shard_map/ppermute | solution.py:45
  187.5 18.6 %early_sum.3 = (f32[512,128]{1,0:T(8,128)S(1)}, s32[80]{0:T(128)S(1)}, s32[16]{0:T(128)S(1)}, s32[48]{0:T(128)S(1)}, s32[16]{0:T(128)S(1)}, /*index=5*/f32[8,128]{1,0:T(8,128)}) custom-call(s32[128]{0:T(128)S(1)} %get-tuple-element.56.order, s32[128]{0:T(128)S(1)} %get-tuple-element.53.skip, s32[256]{0:T(256)S(1)} %reshape_squeeze.3.pos, ...), custom_call_target="tpu_custom_call" | custom-call | flops 1342177280 | bytes 15728640 | tf_op jit(solution)/shard_map/early_sum/pallas_call | solution.py:332
  206.1 8.4 %mid_sum.3.acc_in = f32[512,128]{1,0:T(8,128)S(1)} custom-call(s32[80]{0:T(128)S(1)} %get-tuple-element.21.codes, s32[16]{0:T(128)S(1)} %get-tuple-element.22.off, f32[512,128]{1,0:T(8,128)S(1)} %get-tuple-element.23.acc_in, bf16[128,256,256]{2,1,0:T(8,128)(2,1)} %bitcast.30, bf16[8,528,128]{2,1,0:T(8,128)(2,1)S(1)} %collective-permute-done.26.rest_0_.rest_2_, ...), custom_call_target="tpu_custom_call" | custom-call | flops 536870912 | bytes 6291456 | tf_op jit(solution)/shard_map/mid_sum/pallas_call | solution.py:364
  214.5 5.1 %late_second.1 = (bf16[512,128]{1,0:T(8,128)(2,1)}, f32[2]{0:T(128)}) custom-call(s32[48]{0:T(128)S(1)} %get-tuple-element.19.codes, s32[16]{0:T(128)S(1)} %get-tuple-element.20.off, s32[128]{0:T(128)S(1)} %fusion.2.jtab, f32[512,128]{1,0:T(8,128)S(1)} %mid_sum.3.acc_in, bf16[128,128]{1,0:T(8,128)(2,1)S(1)} %copy-done.5, bf16[128,256,256]{2,1,0:T(8,128)(2,1)} %bitcast.31, ...), custom_call_target="tpu_custom_call" | custom-call | flops 268435456 | bytes 3145728 | tf_op jit(solution)/shard_map/late_second/pallas_call | solution.py:397
  (98 shorter events, 24.5 us)
Async XLA Ops:
  11.8 9.6 %collective-permute-start.3 = (bf16[4,512,128]{2,1,0:T(8,128)(2,1)S(1)}, bf16[4,512,128]{2,1,0:T(8,128)(2,1)S(1)}, u32[]{:S(2)}, u32[]{:S(2)}) collective-permute-start(bf16[4,512,128]{2,1,0:T(8,128)(2,1)S(1)} %pad_maximum_fusion.1), channel_id=1, source_target_pairs={{0,2},{1,3},{2,4},{3,5},{4,6},{5,7},{6,0},{7,1},{8,24},{9,25},{10,... | collective-permute-start | bytes 1572872 | tf_op jit(solution)/shard_map/ppermute | solution.py:45
  13.0 14.9 %collective-permute-start.4 = (bf16[4,512,128]{2,1,0:T(8,128)(2,1)S(1)}, bf16[4,512,128]{2,1,0:T(8,128)(2,1)S(1)}, u32[]{:S(2)}, u32[]{:S(2)}) collective-permute-start(bf16[4,512,128]{2,1,0:T(8,128)(2,1)S(1)} %pad_maximum_fusion.1), channel_id=1, source_target_pairs={{0,4},{1,5},{2,6},{3,7},{4,0},{5,1},{6,2},{7,3},{8,40},{9,41},{10,... | collective-permute-start | bytes 1572872 | tf_op jit(solution)/shard_map/ppermute | solution.py:45
  16.4 11.7 %collective-permute-start.5 = (bf16[4,512,128]{2,1,0:T(8,128)(2,1)S(1)}, bf16[4,512,128]{2,1,0:T(8,128)(2,1)S(1)}, u32[]{:S(2)}, u32[]{:S(2)}) collective-permute-start(bf16[4,512,128]{2,1,0:T(8,128)(2,1)S(1)} %pad_maximum_fusion.1), channel_id=1, source_target_pairs={{0,6},{1,7},{2,0},{3,1},{4,2},{5,3},{6,4},{7,5},{8,56},{9,57},{10,... | collective-permute-start | bytes 1572872 | tf_op jit(solution)/shard_map/ppermute | solution.py:45
  28.4 33.5 %collective-permute-start.6 = (bf16[16,512,128]{2,1,0:T(8,128)(2,1)S(1)}, bf16[16,512,128]{2,1,0:T(8,128)(2,1)S(1)}, u32[]{:S(2)}, u32[]{:S(2)}) collective-permute-start(bf16[16,512,128]{2,1,0:T(8,128)(2,1)S(1)} %get-tuple-element.31.s16), channel_id=1, source_target_pairs={{0,8},{1,9},{2,10},{3,11},{4,12},{5,13},{6,14},{7,15},{8,0},{9,1},... | collective-permute-start | bytes 6291464 | tf_op jit(solution)/shard_map/ppermute | solution.py:49
  31.6 14.0 %collective-permute-start.8 = (bf16[8,512,128]{2,1,0:T(8,128)(2,1)S(1)}, bf16[8,512,128]{2,1,0:T(8,128)(2,1)S(1)}, u32[]{:S(2)}, u32[]{:S(2)}) collective-permute-start(bf16[8,512,128]{2,1,0:T(8,128)(2,1)S(1)} %get-tuple-element.30), channel_id=1, source_target_pairs={{0,48},{1,49},{2,50},{3,51},{4,52},{5,53},{6,54},{7,55},{8,73},{9,... | collective-permute-start | bytes 3145736 | tf_op jit(solution)/shard_map/ppermute | solution.py:45
  33.9 15.3 %collective-permute-start.9 = (bf16[8,512,128]{2,1,0:T(8,128)(2,1)S(1)}, bf16[8,512,128]{2,1,0:T(8,128)(2,1)}, u32[]{:S(2)}, u32[]{:S(2)}) collective-permute-start(bf16[8,512,128]{2,1,0:T(8,128)(2,1)S(1)} %get-tuple-element.30), channel_id=1, source_target_pairs={{0,16},{1,17},{2,18},{3,19},{4,20},{5,21},{6,22},{7,23},{8,72},{9,... | collective-permute-start | bytes 3145736 | tf_op jit(solution)/shard_map/ppermute | solution.py:45
  33.9 26.5 %collective-permute-start.7 = (bf16[8,512,128]{2,1,0:T(8,128)(2,1)S(1)}, bf16[8,512,128]{2,1,0:T(8,128)(2,1)}, u32[]{:S(2)}, u32[]{:S(2)}) collective-permute-start(bf16[8,512,128]{2,1,0:T(8,128)(2,1)S(1)} %get-tuple-element.34), channel_id=1, source_target_pairs={{0,16},{1,17},{2,18},{3,19},{4,20},{5,21},{6,22},{7,23},{8,72},{9,... | collective-permute-start | bytes 3145736 | tf_op jit(solution)/shard_map/ppermute | solution.py:45
  33.9 26.5 %collective-permute-start.10 = (bf16[8,512,128]{2,1,0:T(8,128)(2,1)S(1)}, bf16[8,512,128]{2,1,0:T(8,128)(2,1)}, u32[]{:S(2)}, u32[]{:S(2)}) collective-permute-start(bf16[8,512,128]{2,1,0:T(8,128)(2,1)S(1)} %get-tuple-element.34), channel_id=1, source_target_pairs={{0,48},{1,49},{2,50},{3,51},{4,52},{5,53},{6,54},{7,55},{8,73},{9,... | collective-permute-start | bytes 3145736 | tf_op jit(solution)/shard_map/ppermute | solution.py:45
  45.7 17.5 %collective-permute-start.12 = (bf16[8,512,128]{2,1,0:T(8,128)(2,1)S(1)}, bf16[8,512,128]{2,1,0:T(8,128)(2,1)S(1)}, u32[]{:S(2)}, u32[]{:S(2)}) collective-permute-start(bf16[8,512,128]{2,1,0:T(8,128)(2,1)S(1)} %collective-permute-done.8.rest_1_), channel_id=1, source_target_pairs={{0,8},{1,9},{2,10},{3,11},{4,12},{5,13},{6,14},{7,15},{8,0},{9,1},... | collective-permute-start | bytes 3145736 | tf_op jit(solution)/shard_map/ppermute | solution.py:49
  49.2 19.0 %collective-permute-start.16 = (bf16[8,512,128]{2,1,0:T(8,128)(2,1)S(1)}, bf16[8,512,128]{2,1,0:T(8,128)(2,1)}, u32[]{:S(2)}, u32[]{:S(2)}) collective-permute-start(bf16[8,512,128]{2,1,0:T(8,128)(2,1)S(1)} %collective-permute-done.8.rest_1_), channel_id=1, source_target_pairs={{0,48},{1,49},{2,50},{3,51},{4,52},{5,53},{6,54},{7,55},{8,73},{9,... | collective-permute-start | bytes 3145736 | tf_op jit(solution)/shard_map/ppermute | solution.py:45
  60.4 15.5 %collective-permute-start.15 = (bf16[8,512,128]{2,1,0:T(8,128)(2,1)}, bf16[8,512,128]{2,1,0:T(8,128)(2,1)}, u32[]{:S(2)}, u32[]{:S(2)}) collective-permute-start(bf16[8,512,128]{2,1,0:T(8,128)(2,1)} %collective-permute-done.7.rest_0_), channel_id=1, source_target_pairs={{0,16},{1,17},{2,18},{3,19},{4,20},{5,21},{6,22},{7,23},{8,72},{9,... | collective-permute-start | bytes 3145736 | tf_op jit(solution)/shard_map/ppermute | solution.py:45
  60.4 39.2 %collective-permute-start.11 = (bf16[8,512,128]{2,1,0:T(8,128)(2,1)}, bf16[8,512,128]{2,1,0:T(8,128)(2,1)}, u32[]{:S(2)}, u32[]{:S(2)}) collective-permute-start(bf16[8,512,128]{2,1,0:T(8,128)(2,1)} %collective-permute-done.7.rest_0_), channel_id=1, source_target_pairs={{0,8},{1,9},{2,10},{3,11},{4,12},{5,13},{6,14},{7,15},{8,0},{9,1},... | collective-permute-start | bytes 3145736 | tf_op jit(solution)/shard_map/ppermute | solution.py:49
  63.2 36.5 %collective-permute-start.13 = (bf16[8,512,128]{2,1,0:T(8,128)(2,1)}, bf16[8,512,128]{2,1,0:T(8,128)(2,1)}, u32[]{:S(2)}, u32[]{:S(2)}) collective-permute-start(bf16[8,512,128]{2,1,0:T(8,128)(2,1)} %collective-permute-done.9.rest_2_), channel_id=1, source_target_pairs={{0,8},{1,9},{2,10},{3,11},{4,12},{5,13},{6,14},{7,15},{8,0},{9,1},... | collective-permute-start | bytes 3145736 | tf_op jit(solution)/shard_map/ppermute | solution.py:49
  64.2 35.5 %collective-permute-start.14 = (bf16[8,512,128]{2,1,0:T(8,128)(2,1)}, bf16[8,512,128]{2,1,0:T(8,128)(2,1)}, u32[]{:S(2)}, u32[]{:S(2)}) collective-permute-start(bf16[8,512,128]{2,1,0:T(8,128)(2,1)} %collective-permute-done.10.rest_3_), channel_id=1, source_target_pairs={{0,8},{1,9},{2,10},{3,11},{4,12},{5,13},{6,14},{7,15},{8,0},{9,1},... | collective-permute-start | bytes 3145736 | tf_op jit(solution)/shard_map/ppermute | solution.py:49
  68.2 40.4 %collective-permute-start.18 = (bf16[8,512,128]{2,1,0:T(8,128)(2,1)}, bf16[8,512,128]{2,1,0:T(8,128)(2,1)}, u32[]{:S(2)}, u32[]{:S(2)}) collective-permute-start(bf16[8,512,128]{2,1,0:T(8,128)(2,1)} %collective-permute-done.16.rest_1_), channel_id=1, source_target_pairs={{0,8},{1,9},{2,10},{3,11},{4,12},{5,13},{6,14},{7,15},{8,0},{9,1},... | collective-permute-start | bytes 3145736 | tf_op jit(solution)/shard_map/ppermute | solution.py:49
  75.9 32.7 %collective-permute-start.17 = (bf16[8,512,128]{2,1,0:T(8,128)(2,1)}, bf16[8,512,128]{2,1,0:T(8,128)(2,1)}, u32[]{:S(2)}, u32[]{:S(2)}) collective-permute-start(bf16[8,512,128]{2,1,0:T(8,128)(2,1)} %collective-permute-done.15.rest_0_), channel_id=1, source_target_pairs={{0,8},{1,9},{2,10},{3,11},{4,12},{5,13},{6,14},{7,15},{8,0},{9,1},... | collective-permute-start | bytes 3145736 | tf_op jit(solution)/shard_map/ppermute | solution.py:49
  123.8 15.6 %collective-permute-start.22 = (bf16[4,528,128]{2,1,0:T(8,128)(2,1)S(1)}, bf16[4,528,128]{2,1,0:T(8,128)(2,1)S(1)}, u32[]{:S(2)}, u32[]{:S(2)}) collective-permute-start(bf16[4,528,128]{2,1,0:T(8,128)(2,1)S(1)} %pad_maximum_fusion), channel_id=1, source_target_pairs={{0,2},{1,3},{2,4},{3,5},{4,6},{5,7},{6,0},{7,1},{8,24},{9,25},{10,... | collective-permute-start | bytes 1622024 | tf_op jit(solution)/shard_map/ppermute | solution.py:45
  123.9 15.7 %collective-permute-start.23 = (bf16[4,528,128]{2,1,0:T(8,128)(2,1)S(1)}, bf16[4,528,128]{2,1,0:T(8,128)(2,1)S(1)}, u32[]{:S(2)}, u32[]{:S(2)}) collective-permute-start(bf16[4,528,128]{2,1,0:T(8,128)(2,1)S(1)} %pad_maximum_fusion), channel_id=1, source_target_pairs={{0,4},{1,5},{2,6},{3,7},{4,0},{5,1},{6,2},{7,3},{8,40},{9,41},{10,... | collective-permute-start | bytes 1622024 | tf_op jit(solution)/shard_map/ppermute | solution.py:45
  124.7 15.3 %collective-permute-start.24 = (bf16[4,528,128]{2,1,0:T(8,128)(2,1)S(1)}, bf16[4,528,128]{2,1,0:T(8,128)(2,1)S(1)}, u32[]{:S(2)}, u32[]{:S(2)}) collective-permute-start(bf16[4,528,128]{2,1,0:T(8,128)(2,1)S(1)} %pad_maximum_fusion), channel_id=1, source_target_pairs={{0,6},{1,7},{2,0},{3,1},{4,2},{5,3},{6,4},{7,5},{8,56},{9,57},{10,... | collective-permute-start | bytes 1622024 | tf_op jit(solution)/shard_map/ppermute | solution.py:45
  140.2 31.8 %collective-permute-start.25 = (bf16[16,528,128]{2,1,0:T(8,128)(2,1)S(1)}, bf16[16,528,128]{2,1,0:T(8,128)(2,1)S(1)}, u32[]{:S(2)}, u32[]{:S(2)}) collective-permute-start(bf16[16,528,128]{2,1,0:T(8,128)(2,1)S(1)} %get-tuple-element.25.s16.rest_0_), channel_id=1, source_target_pairs={{0,8},{1,9},{2,10},{3,11},{4,12},{5,13},{6,14},{7,15},{8,0},{9,1},... | collective-permute-start | bytes 6488072 | tf_op jit(solution)/shard_map/ppermute | solution.py:49
  142.9 14.5 %collective-permute-start.27 = (bf16[8,528,128]{2,1,0:T(8,128)(2,1)S(1)}, bf16[8,528,128]{2,1,0:T(8,128)(2,1)S(1)}, u32[]{:S(2)}, u32[]{:S(2)}) collective-permute-start(bf16[8,528,128]{2,1,0:T(8,128)(2,1)S(1)} %get-tuple-element.24), channel_id=1, source_target_pairs={{0,48},{1,49},{2,50},{3,51},{4,52},{5,53},{6,54},{7,55},{8,73},{9,... | collective-permute-start | bytes 3244040 | tf_op jit(solution)/shard_map/ppermute | solution.py:45
  145.3 15.5 %collective-permute-start.28 = (bf16[8,528,128]{2,1,0:T(8,128)(2,1)S(1)}, bf16[8,528,128]{2,1,0:T(8,128)(2,1)S(1)}, u32[]{:S(2)}, u32[]{:S(2)}) collective-permute-start(bf16[8,528,128]{2,1,0:T(8,128)(2,1)S(1)} %get-tuple-element.24), channel_id=1, source_target_pairs={{0,16},{1,17},{2,18},{3,19},{4,20},{5,21},{6,22},{7,23},{8,72},{9,... | collective-permute-start | bytes 3244040 | tf_op jit(solution)/shard_map/ppermute | solution.py:45
  145.3 26.8 %collective-permute-start.26 = (bf16[8,528,128]{2,1,0:T(8,128)(2,1)S(1)}, bf16[8,528,128]{2,1,0:T(8,128)(2,1)S(1)}, u32[]{:S(2)}, u32[]{:S(2)}) collective-permute-start(bf16[8,528,128]{2,1,0:T(8,128)(2,1)S(1)} %get-tuple-element.28), channel_id=1, source_target_pairs={{0,16},{1,17},{2,18},{3,19},{4,20},{5,21},{6,22},{7,23},{8,72},{9,... | collective-permute-start | bytes 3244040 | tf_op jit(solution)/shard_map/ppermute | solution.py:45
  145.3 26.8 %collective-permute-start.29 = (bf16[8,528,128]{2,1,0:T(8,128)(2,1)S(1)}, bf16[8,528,128]{2,1,0:T(8,128)(2,1)S(1)}, u32[]{:S(2)}, u32[]{:S(2)}) collective-permute-start(bf16[8,528,128]{2,1,0:T(8,128)(2,1)S(1)} %get-tuple-element.28), channel_id=1, source_target_pairs={{0,48},{1,49},{2,50},{3,51},{4,52},{5,53},{6,54},{7,55},{8,73},{9,... | collective-permute-start | bytes 3244040 | tf_op jit(solution)/shard_map/ppermute | solution.py:45
  157.4 15.2 %collective-permute-start.31 = (bf16[8,528,128]{2,1,0:T(8,128)(2,1)S(1)}, bf16[8,528,128]{2,1,0:T(8,128)(2,1)S(1)}, u32[]{:S(2)}, u32[]{:S(2)}) collective-permute-start(bf16[8,528,128]{2,1,0:T(8,128)(2,1)S(1)} %collective-permute-done.27.rest_1_.rest_3_), channel_id=1, source_target_pairs={{0,8},{1,9},{2,10},{3,11},{4,12},{5,13},{6,14},{7,15},{8,0},{9,1},... | collective-permute-start | bytes 3244040 | tf_op jit(solution)/shard_map/ppermute | solution.py:49
  160.8 19.8 %collective-permute-start.35 = (bf16[8,528,128]{2,1,0:T(8,128)(2,1)S(1)}, bf16[8,528,128]{2,1,0:T(8,128)(2,1)S(1)}, u32[]{:S(2)}, u32[]{:S(2)}) collective-permute-start(bf16[8,528,128]{2,1,0:T(8,128)(2,1)S(1)} %collective-permute-done.27.rest_1_.rest_3_), channel_id=1, source_target_pairs={{0,48},{1,49},{2,50},{3,51},{4,52},{5,53},{6,54},{7,55},{8,73},{9,... | collective-permute-start | bytes 3244040 | tf_op jit(solution)/shard_map/ppermute | solution.py:45
  172.1 15.2 %collective-permute-start.34 = (bf16[8,528,128]{2,1,0:T(8,128)(2,1)S(1)}, bf16[8,528,128]{2,1,0:T(8,128)(2,1)S(1)}, u32[]{:S(2)}, u32[]{:S(2)}) collective-permute-start(bf16[8,528,128]{2,1,0:T(8,128)(2,1)S(1)} %collective-permute-done.26.rest_0_.rest_2_), channel_id=1, source_target_pairs={{0,16},{1,17},{2,18},{3,19},{4,20},{5,21},{6,22},{7,23},{8,72},{9,... | collective-permute-start | bytes 3244040 | tf_op jit(solution)/shard_map/ppermute | solution.py:45
  172.1 34.0 %collective-permute-start.30 = (bf16[8,528,128]{2,1,0:T(8,128)(2,1)S(1)}, bf16[8,528,128]{2,1,0:T(8,128)(2,1)S(1)}, u32[]{:S(2)}, u32[]{:S(2)}) collective-permute-start(bf16[8,528,128]{2,1,0:T(8,128)(2,1)S(1)} %collective-permute-done.26.rest_0_.rest_2_), channel_id=1, source_target_pairs={{0,8},{1,9},{2,10},{3,11},{4,12},{5,13},{6,14},{7,15},{8,0},{9,1},... | collective-permute-start | bytes 3244040 | tf_op jit(solution)/shard_map/ppermute | solution.py:49
  172.1 34.0 %collective-permute-start.32 = (bf16[8,528,128]{2,1,0:T(8,128)(2,1)S(1)}, bf16[8,528,128]{2,1,0:T(8,128)(2,1)S(1)}, u32[]{:S(2)}, u32[]{:S(2)}) collective-permute-start(bf16[8,528,128]{2,1,0:T(8,128)(2,1)S(1)} %collective-permute-done.28.rest_2_.rest_4_), channel_id=1, source_target_pairs={{0,8},{1,9},{2,10},{3,11},{4,12},{5,13},{6,14},{7,15},{8,0},{9,1},... | collective-permute-start | bytes 3244040 | tf_op jit(solution)/shard_map/ppermute | solution.py:49
  172.6 33.5 %collective-permute-start.33 = (bf16[8,528,128]{2,1,0:T(8,128)(2,1)S(1)}, bf16[8,528,128]{2,1,0:T(8,128)(2,1)S(1)}, u32[]{:S(2)}, u32[]{:S(2)}) collective-permute-start(bf16[8,528,128]{2,1,0:T(8,128)(2,1)S(1)} %collective-permute-done.29.rest_3_.rest_5_), channel_id=1, source_target_pairs={{0,8},{1,9},{2,10},{3,11},{4,12},{5,13},{6,14},{7,15},{8,0},{9,1},... | collective-permute-start | bytes 3244040 | tf_op jit(solution)/shard_map/ppermute | solution.py:49
  180.5 34.0 %collective-permute-start.37 = (bf16[8,528,128]{2,1,0:T(8,128)(2,1)S(1)}, bf16[8,528,128]{2,1,0:T(8,128)(2,1)S(1)}, u32[]{:S(2)}, u32[]{:S(2)}) collective-permute-start(bf16[8,528,128]{2,1,0:T(8,128)(2,1)S(1)} %collective-permute-done.35.rest_11_), channel_id=1, source_target_pairs={{0,8},{1,9},{2,10},{3,11},{4,12},{5,13},{6,14},{7,15},{8,0},{9,1},... | collective-permute-start | bytes 3244040 | tf_op jit(solution)/shard_map/ppermute | solution.py:49
  187.3 27.2 %collective-permute-start.36 = (bf16[8,528,128]{2,1,0:T(8,128)(2,1)S(1)}, bf16[8,528,128]{2,1,0:T(8,128)(2,1)S(1)}, u32[]{:S(2)}, u32[]{:S(2)}) collective-permute-start(bf16[8,528,128]{2,1,0:T(8,128)(2,1)S(1)} %collective-permute-done.34.rest_10_), channel_id=1, source_target_pairs={{0,8},{1,9},{2,10},{3,11},{4,12},{5,13},{6,14},{7,15},{8,0},{9,1},... | collective-permute-start | bytes 3244040 | tf_op jit(solution)/shard_map/ppermute | solution.py:49
  (20 other events, 531.8 us)
where the time goes:
time: 221 us; the launch traced here: 220 us
  waiting for transfers between devices  99.3 us (45%)
  Pallas kernels  67.4 us (30%)
  starting transfers between devices  44.1 us (20%)
  local copies, waits for them, and re-layouts  6.58 us (3%)
    ppermute x24, waiting for transfers between devices, shift(): return lax.ppermute(value, AXES, PERM[stage, k])  99.3 us
    pallas_call x2, Pallas kernels, early(): pl.pallas_call(early_kernel, out_shape=(jax.ShapeDtypeStruct((ROWS, W), j...  38.2 us
    ppermute x24, starting transfers between devices, shift(): return lax.ppermute(value, AXES, PERM[stage, k])  29.6 us
    pallas_call x2, Pallas kernels, mid_sum(): pl.pallas_call(mid_kernel, out_shape=jax.ShapeDtypeStruct((ROWS, W), jnp....  17.2 us
    ppermute x14, starting transfers between devices, swap(): return lax.ppermute(value, AXES, SWAP)  14.6 us
    pallas_call x1, Pallas kernels, late_first(): pl.pallas_call(late_first_kernel, out_shape=jax.ShapeDtypeStruct((ROWS +...  7 us
    unnamed x39, local copies, waits for them, and re-layouts  5.61 us
    pallas_call x1, Pallas kernels, late_second(): pl.pallas_call(late_second_kernel, out_shape=(jax.ShapeDtypeStruct((ROWS,...  5.08 us
  transfers between devices with their start and end apart: 38, of which 19 were waited for; matrix products, arithmetic and copies ran while one was open for 1% of the time, Pallas kernels for 25%

commit v1 on v0

v1 whole, which is shorter than its diff:
```python
import functools

import jax
import jax.numpy as jnp
from jax import lax
from jax.experimental import pallas as pl
from jax.experimental.pallas import tpu as pltpu
from jax.sharding import Mesh
from jax.sharding import PartitionSpec as P


AXES = ("ylo", "x", "core", "z", "yhi")
NB = 128
ROWS = 512
TS = 256
W = 128
UNROLL = 4
AX = ((1, 2, 0), (0, 2, 1))
QA = [(k, 0) for k in range(4)]
QB = [(k, 1) for k in range(4)] + [(k, 3) for k in range(4)]
QC = [(k, 2) for k in range(4)]
GROUPS = (
    ((QA, 0), (QA, 1), (QA, 3), (QA, 2), (QB, 0), (QC, 0)),
    ((QB, 1), (QB, 3)),
    ((QC, 1), (QC, 3), (QB, 2), (QC, 2)),
)


def sizes(group):
    return [len(q) for q, _ in GROUPS[group]]


def coords(i):
    return [(i // 16) % 4, (i % 2) * 2 + i // 64, (i // 2) % 4, (i // 8) % 2]


def block_id(x, y, z, core):
    return (y % 2) * 64 + x * 16 + core * 8 + z * 2 + y // 2


def stage_perm(stage, shift):
    pairs = []
    for i in range(NB):
        c = coords(i)
        a = AX[c[3]][stage]
        c[a] = (c[a] + shift) % 4
        pairs.append((i, block_id(*c)))
    return pairs


PERM = {(s, k): stage_perm(s, k) for s in range(3) for k in (1, 2, 3)}
SWAP = [(i, i ^ 8) for i in range(NB)]


def shift(value, stage, k):
    return lax.ppermute(value, AXES, PERM[(stage, k)])


def swap(value):
    return lax.ppermute(value, AXES, SWAP)


def gather(block):
    s1 = block[None]
    qa = jnp.concatenate([s1] + [shift(s1, 0, k) for k in (1, 2, 3)], 0)
    q1, q3, q2 = (shift(qa, 1, k) for k in (1, 3, 2))
    ap = shift(qa, 2, 1)
    am = shift(qa, 2, 3)
    fa = shift(ap, 2, 1)
    qb = jnp.concatenate([q1, q3], 0)
    bp = shift(qb, 2, 1)
    bm = shift(qb, 2, 3)
    fb = shift(bm, 2, 3)
    cp = shift(q2, 2, 1)
    cm = shift(q2, 2, 3)
    fc = shift(cp, 2, 1)
    return [qa, ap, am, fa, qb, q2], [bp, bm], [cp, cm, fb, fc]


def item_blocks():
    k1, k2, k3 = [], [], []
    for group in GROUPS:
        for slots, third in group:
            for first, second in slots:
                k1.append(first)
                k2.append(second)
                k3.append(third)
    k1, k2, k3 = (jnp.array(v, jnp.int32) for v in (k1, k2, k3))
    core = lax.axis_index("core")
    y = lax.axis_index("yhi") * 2 + lax.axis_index("ylo")
    zero = core == 0
    bx = (lax.axis_index("x") - jnp.where(zero, k3, k1)) & 3
    by = (y - jnp.where(zero, k1, k3)) & 3
    bz = (lax.axis_index("z") - k2) & 3
    return (by & 1) * 64 + bx * 16 + core * 8 + bz * 2 + (by >> 1)


PADDING = 4


def groups_of(n):
    return (n + (UNROLL - 1)) // UNROLL


def pad(ref, n):
    for u in range(UNROLL - 1):
        ref[n + u] = PADDING


def half_rows(code):
    return pl.ds(((code >> 3) & 1) * TS, TS)


def start_tile(tiles, other, tbuf, tsem, code, slot):
    block = (code >> 4) & 127
    theirs = (code >> 1) & 1

    @pl.when(theirs == 0)
    def _():
        pltpu.make_async_copy(tiles.at[block], tbuf.at[slot], tsem.at[slot]).start()

    @pl.when(theirs == 1)
    def _():
        pltpu.make_async_copy(other.at[block], tbuf.at[slot], tsem.at[slot]).start()


def wait_tile(tiles, tbuf, tsem, slot):
    pltpu.make_async_copy(tiles.at[0], tbuf.at[slot], tsem.at[slot]).wait()


def run(n, start, wait, source, codes, accs, tbuf):
    depth = tbuf.shape[0]
    total = groups_of(n) * UNROLL

    def prime(t, c):
        start(t, t)
        return c

    lax.fori_loop(0, jnp.minimum(total, depth), prime, 0)

    def body(g, c):
        first = g * UNROLL
        slot0 = first & (depth - 1)
        for u in range(UNROLL):
            wait(first + u, slot0 + u)
        for u in range(UNROLL):
            rows = pl.ds((codes[first + u] & 7) * TS, TS)
            accs[u, rows, :] += jnp.dot(
                tbuf[slot0 + u],
                source(first + u, slot0 + u),
                preferred_element_type=jnp.float32,
            )

        @pl.when(first + depth < total)
        def _():
            for u in range(UNROLL):
                start(first + u + depth, slot0 + u)

        return c

    lax.fori_loop(0, groups_of(n), body, 0)


def run_staged(n, codes, accs, tiles, other, tbuf, tsem, stage):
    run(
        n,
        lambda t, slot: start_tile(tiles, other, tbuf, tsem, codes[t], slot),
        lambda t, slot: wait_tile(tiles, tbuf, tsem, slot),
        lambda t, slot: stage[t],
        codes,
        accs,
        tbuf,
    )


def fill_stage(codes, first, last, ref, stage):
    def body(t, c):
        code = codes[t]
        stage[t] = ref[code >> 16, half_rows(code), :]
        return c

    lax.fori_loop(first, last, body, 0)


def total_of(accs, first, rows):
    total = accs[0, first : first + rows, :]
    for u in range(1, UNROLL):
        total = total + accs[u, first : first + rows, :]
    return total


def early_kernel(
    order, skip, pos, pos2, jtab, own, tiles, cached, block,
    acc, list1, off1, list2, off2, list3, off3, drift,
    clist, flags, accs, tbuf, sbuf, own_buf, tsem, ssem, osem,
):
    me = own[0]
    own_copy = pltpu.make_async_copy(cached.at[me], own_buf, osem)
    own_copy.start()

    def set_flag(r, c):
        flags[order[r]] = 1 - skip[r]
        return c

    lax.fori_loop(0, NB, set_flag, 0)

    def stale(j, n):
        clist[n] = (j << 4) | (pos[2 * j + 1] << 3) | pos[2 * j]
        return n + jnp.where((flags[j] == 0) & (j != me), 1, 0)

    nc = lax.fori_loop(0, NB, stale, 0)
    pad(clist, nc)

    def split(first, last, n, out):
        def build(t, n):
            j = jtab[t]
            fresh = flags[j]
            low = ((t - first) << 16) | (j << 4)
            out[n] = low | (pos[2 * j + 1] << 3) | pos[2 * j]
            n = n + jnp.where((fresh == 1) | (j == me), 1, 0)
            out[n] = low | (pos2[2 * j + 1] << 3) | 2 | pos2[2 * j]
            return n + fresh

        return lax.fori_loop(first, last, build, n)

    base = 0
    for group, (out, off) in enumerate(((list1, off1), (list2, off2), (list3, off3))):
        n = 0
        for p, size in enumerate(sizes(group)):
            off[p] = n
            n = split(base, base + size, n, out)
            base += size
        off[len(sizes(group))] = n
        pad(out, n)
    accs[...] = jnp.zeros_like(accs)

    def source_copy(t, slot):
        code = clist[t]
        return pltpu.make_async_copy(
            cached.at[(code >> 4) & 127, half_rows(code), :], sbuf.at[slot], ssem.at[slot]
        )

    def tile_copy(t, slot):
        return pltpu.make_async_copy(
            tiles.at[(clist[t] >> 4) & 127], tbuf.at[slot], tsem.at[slot]
        )

    def start(t, slot):
        tile_copy(t, slot).start()
        source_copy(t, slot).start()

    def wait(t, slot):
        tile_copy(t, slot).wait()
        source_copy(t, slot).wait()

    run(nc, start, wait, lambda t, slot: sbuf[slot], clist, accs, tbuf)
    acc[...] = total_of(accs, 0, ROWS)
    own_copy.wait()
    diff = block[0:ROWS, :].astype(jnp.float32) - own_buf[...].astype(jnp.float32)
    drift[...] = jnp.broadcast_to(jnp.sum(diff * diff, axis=0, keepdims=True), (8, W))


def add_pieces(codes, off, tiles, other, pieces, accs, tbuf, stage, tsem):
    accs[...] = jnp.zeros_like(accs)
    for p, ref in enumerate(pieces):
        fill_stage(codes, off[p], off[p + 1], ref, stage)
    run_staged(off[len(pieces)], codes, accs, tiles, other, tbuf, tsem, stage)


def mid_kernel(codes, off, acc_in, tiles, other, *rest):
    acc, accs, tbuf, stage, tsem = rest[-5:]
    add_pieces(codes, off, tiles, other, rest[:-5], accs, tbuf, stage, tsem)
    have = acc_in.shape[0]
    acc[0:have, :] = acc_in[...] + total_of(accs, 0, have)
    if have < 2 * ROWS:
        acc[have:, :] = total_of(accs, have, 2 * ROWS - have)


def late_kernel(codes, off, jtab, acc_in, tiles, other, *rest, drifts):
    if drifts:
        mine, theirs, accs, tbuf, stage, ext, tsem = rest[-7:]
        pieces = rest[:-7]
    else:
        mine, theirs, accs, tbuf, stage, tsem = rest[-6:]
        pieces = rest[:-6]
    late = len(sizes(2))
    add_pieces(codes, off, tiles, other, pieces[-late:], accs, tbuf, stage, tsem)
    mine[0:ROWS, :] = acc_in[0:ROWS, :] + total_of(accs, 0, ROWS)
    theirs[0:ROWS, :] = acc_in[ROWS:, :] + total_of(accs, ROWS, ROWS)
    if drifts:
        base = 0
        for ref in pieces:
            for s in range(ref.shape[0]):
                ext[jtab[base + s]] = ref[s, ROWS:, :].astype(jnp.float32)
            base += ref.shape[0]
        core = (jtab[0] >> 3) & 1
        total = jnp.zeros((16, W), jnp.float32)
        for hi in range(8):
            total = total + jnp.sum(ext[pl.ds(hi * 16 + core * 8, 8)], axis=0)
        mine[ROWS:, :] = total
        theirs[ROWS:, :] = total


def split3(row):
    hi = row.astype(jnp.bfloat16).astype(jnp.float32)
    mid = (row - hi).astype(jnp.bfloat16).astype(jnp.float32)
    return hi, mid, row - hi - mid


def finish_first_kernel(own, mine, theirs, drift_in, weight, cached, payload, own_buf, osem):
    own_copy = pltpu.make_async_copy(cached.at[own[0]], own_buf, osem)
    own_copy.start()
    total = mine[...] + theirs[...]
    hidden = jnp.maximum(
        jnp.dot(
            total.astype(jnp.bfloat16), weight[...], preferred_element_type=jnp.float32
        ),
        0.0,
    ).astype(jnp.bfloat16)
    payload[0:ROWS, :] = hidden
    own_copy.wait()
    diff = hidden.astype(jnp.float32) - own_buf[...].astype(jnp.float32)
    second = jnp.sum(diff * diff, axis=0, keepdims=True)
    row = lax.broadcasted_iota(jnp.int32, (16, W), 0)
    extra = jnp.zeros((16, W), jnp.float32)
    for k, part in enumerate(split3(drift_in[0:1, :]) + split3(second)):
        extra = jnp.where(row == k, jnp.broadcast_to(part, (16, W)), extra)
    payload[ROWS:, :] = extra.astype(jnp.bfloat16)


def finish_second_kernel(mine, theirs, weight, output, drift):
    total = mine[0:ROWS, :] + theirs[0:ROWS, :]
    output[...] = jnp.dot(
        total.astype(jnp.bfloat16), weight[...], preferred_element_type=jnp.float32
    ).astype(jnp.bfloat16)
    parts = mine[ROWS:, :] + theirs[ROWS:, :]
    cells = 1.0 / (NB * ROWS * W)
    drift[0] = jnp.sum(parts[0:3, :]) * cells
    drift[1] = jnp.sum(parts[3:6, :]) * cells


SMEM = pl.BlockSpec(memory_space=pltpu.SMEM)
VMEM = pl.BlockSpec(memory_space=pltpu.VMEM)
HBM = pl.BlockSpec(memory_space=pltpu.HBM)
ACCS = pltpu.VMEM((UNROLL, 5 * TS, W), jnp.float32)
BLOCK = pltpu.VMEM((ROWS, W), jnp.bfloat16)


def ring_of(depth):
    return [pltpu.VMEM((depth, TS, TS), jnp.bfloat16)]


def sems_of(depth):
    return pltpu.SemaphoreType.DMA((depth,))


def stage_of(blocks):
    return pltpu.VMEM((2 * blocks + UNROLL, TS, W), jnp.bfloat16)


def params(mib):
    return pltpu.CompilerParams(vmem_limit_bytes=mib * 1024 * 1024)


def cost(items):
    return pl.CostEstimate(
        flops=items * 2 * TS * TS * W, transcendentals=0, bytes_accessed=items * 196608
    )


def list_shapes():
    shapes = []
    for group in (0, 1, 2):
        shapes.append(jax.ShapeDtypeStruct((2 * sum(sizes(group)) + 8,), jnp.int32))
        shapes.append(jax.ShapeDtypeStruct((8,), jnp.int32))
    return shapes


def early(order, skip, pos, pos2, jtab, own, tiles, cached, block):
    return pl.pallas_call(
        early_kernel,
        out_shape=(
            jax.ShapeDtypeStruct((ROWS, W), jnp.float32),
            *list_shapes(),
            jax.ShapeDtypeStruct((8, W), jnp.float32),
        ),
        in_specs=[SMEM] * 6 + [HBM] * 2 + [VMEM],
        out_specs=(VMEM, *[SMEM] * 6, VMEM),
        scratch_shapes=[
            pltpu.SMEM((NB + 8,), jnp.int32),
            pltpu.SMEM((NB,), jnp.int32),
            ACCS,
            *ring_of(32),
            pltpu.VMEM((32, TS, W), jnp.bfloat16),
            BLOCK,
            sems_of(32),
            sems_of(32),
            pltpu.SemaphoreType.DMA,
        ],
        compiler_params=params(16),
        cost_estimate=cost(72),
        name="early_sum",
    )(order, skip, pos, pos2, jtab, own, tiles, cached, block)


def mid_sum(group, codes, off, acc, tiles, other, pieces):
    blocks = sum(sizes(group))
    return pl.pallas_call(
        mid_kernel,
        out_shape=jax.ShapeDtypeStruct((2 * ROWS, W), jnp.float32),
        in_specs=[SMEM] * 2 + [VMEM] + [HBM] * 2 + [VMEM] * len(pieces),
        out_specs=VMEM,
        scratch_shapes=[ACCS, *ring_of(32), stage_of(blocks), sems_of(32)],
        compiler_params=params(20),
        cost_estimate=cost(blocks),
    )(codes, off, acc, tiles, other, *pieces)


def late_sum(codes, off, jtab, acc, tiles, other, pieces, drifts):
    blocks = sum(sizes(2))
    rows = ROWS + 16 if drifts else ROWS
    extra = [pltpu.VMEM((NB, 16, W), jnp.float32)] if drifts else []
    return pl.pallas_call(
        functools.partial(late_kernel, drifts=drifts),
        out_shape=(jax.ShapeDtypeStruct((rows, W), jnp.float32),) * 2,
        in_specs=[SMEM] * 3 + [VMEM] + [HBM] * 2 + [VMEM] * len(pieces),
        out_specs=(VMEM, VMEM),
        scratch_shapes=[ACCS, *ring_of(32), stage_of(blocks), *extra, sems_of(32)],
        compiler_params=params(20),
        cost_estimate=cost(blocks),
        name="late_sum",
    )(codes, off, jtab, acc, tiles, other, *pieces)


def finish_first(own, mine, theirs, drift, weight, cached):
    return pl.pallas_call(
        finish_first_kernel,
        out_shape=jax.ShapeDtypeStruct((ROWS + 16, W), jnp.bfloat16),
        in_specs=[SMEM] + [VMEM] * 4 + [HBM],
        out_specs=VMEM,
        scratch_shapes=[BLOCK, pltpu.SemaphoreType.DMA],
        compiler_params=params(8),
        cost_estimate=cost(1),
        name="finish_first",
    )(own, mine, theirs, drift, weight, cached)


def finish_second(mine, theirs, weight):
    return pl.pallas_call(
        finish_second_kernel,
        out_shape=(
            jax.ShapeDtypeStruct((ROWS, W), jnp.bfloat16),
            jax.ShapeDtypeStruct((2,), jnp.float32),
        ),
        in_specs=[VMEM] * 3,
        out_specs=(VMEM, SMEM),
        compiler_params=params(8),
        cost_estimate=cost(1),
        name="finish_second",
    )(mine, theirs, weight)


def in_hbm(value):
    return pltpu.with_memory_space_constraint(value, pltpu.HBM)


def layer(block, order, skip, pos, pos2, jtab, own, tiles, other, cached, drifts):
    mid0, mid1, late = gather(block)
    acc, list1, off1, list2, off2, list3, off3, drift = early(
        order, skip, pos, pos2, jtab, own, tiles, cached, block
    )
    acc = mid_sum(0, list1, off1, acc, tiles, other, mid0)
    acc = mid_sum(1, list2, off2, acc, tiles, other, mid1)
    pieces = mid0 + mid1 + late if drifts else late
    mine, theirs = late_sum(list3, off3, jtab, acc, tiles, other, pieces, drifts)
    return mine, swap(theirs), drift


def on_device(features, cache_in, cache_hidden, tiles, tile_pos, order, skip, w_first, w_second):
    pos = tile_pos[0].reshape(2 * NB)
    own = lax.axis_index(AXES)[None].astype(jnp.int32)
    jtab = item_blocks()
    cache_in = in_hbm(cache_in.reshape(NB, ROWS, W))
    cache_hidden = in_hbm(cache_hidden.reshape(NB, ROWS, W))
    pos2 = swap(pos)
    other = in_hbm(swap(tiles[0]))
    tiles = in_hbm(tiles[0])
    mine, theirs, drift = layer(
        features, order[0], skip[0], pos, pos2, jtab, own, tiles, other, cache_in, False
    )
    payload = finish_first(own, mine, theirs, drift, w_first, cache_hidden)
    mine, theirs, _ = layer(
        payload, order[1], skip[1], pos, pos2, jtab, own, tiles, other, cache_hidden, True
    )
    return finish_second(mine, theirs, w_second)


def solution(mesh):
    split = Mesh(mesh.devices.reshape(2, 4, 2, 4, 2), AXES)
    both = AXES
    in_specs = (
        P(both, None),
        P(),
        P(),
        P(both, None, None, None),
        P(both, None, None),
        P(),
        P(),
        P(),
        P(),
    )
    out_specs = (P(both, None), P())
    return jax.shard_map(
        on_device, mesh=split, in_specs=in_specs, out_specs=out_specs, check_vma=False
    )
```

time: 221 us -> 177 us (0.80)
  waiting for transfers between devices: 99.3 us -> 73.8 us
  Pallas kernels: 67.4 us -> 55.3 us
  local copies, waits for them, and re-layouts: 6.58 us -> 1.32 us
    ppermute x24 -> x30, waiting for transfers between devices: 99.3 us -> 70.4 us  [shift(): return lax.ppermute(value, AXES, PERM[stage, k])]
    pallas_call x2, Pallas kernels: 38.2 us -> 24.2 us  [early(): pl.pallas_call(early_kernel, out_shape=(jax.ShapeDtypeStruct((ROWS, W), j...]
    ppermute x24 -> x30, starting transfers between devices: 29.6 us -> 40.3 us  [shift(): return lax.ppermute(value, AXES, PERM[stage, k])]
    ppermute x14 -> x4, starting transfers between devices: 14.6 us -> 4.05 us  [swap(): return lax.ppermute(value, AXES, SWAP)]
    unnamed x39 -> x25, local copies, waits for them, and re-layouts: 5.61 us -> 1.04 us
    ppermute x14 -> x4, waiting for transfers between devices: 0.04 us -> 3.32 us  [swap(): return lax.ppermute(value, AXES, SWAP)]
    pallas_call x4 -> x8, Pallas kernels: 29.3 us -> 31.1 us  [the longest x4 19.8 us: mid_sum(): pl.pallas_call(mid_kernel, out_shape=jax.ShapeDtypeStruct((2 * ROWS, W),...]
  transfers between devices with their start and end apart: 38 -> 34, of which waited for: 19 -> 17; matrix products, arithmetic and copies ran while one was open for 1% -> 1% of each run, Pallas kernels for 25% -> 25%
where the time goes in v1:
time: 177 us
  waiting for transfers between devices  73.8 us (42%)
  Pallas kernels  55.3 us (31%)
  starting transfers between devices  44.4 us (25%)
    ppermute x30, waiting for transfers between devices, shift(): return lax.ppermute(value, AXES, PERM[stage, k])  70.4 us
    ppermute x30, starting transfers between devices, shift(): return lax.ppermute(value, AXES, PERM[stage, k])  40.3 us
    pallas_call x2, Pallas kernels, early(): pl.pallas_call(early_kernel, out_shape=(jax.ShapeDtypeStruct((ROWS, W), j...  24.2 us
    pallas_call x4, Pallas kernels, mid_sum(): pl.pallas_call(mid_kernel, out_shape=jax.ShapeDtypeStruct((2 * ROWS, W),...  19.8 us
    pallas_call x2, Pallas kernels, late_sum(): pl.pallas_call(functools.partial(late_kernel, drifts=drifts), out_shape=(...  9.45 us
    ppermute x4, starting transfers between devices, swap(): return lax.ppermute(value, AXES, SWAP)  4.05 us
  transfers between devices with their start and end apart: 34, of which 17 were waited for; matrix products, arithmetic and copies ran while one was open for 1% of the time, Pallas kernels for 25%

profile of v1, /device:TPU:1, one launch (start us, length us, event | category | flops | bytes accessed | tf_op | source)
XLA Modules:
  0.0 176.9 jit_solution(5853640375548511066)
XLA Ops:
  2.1 2.6 %collective-permute-start.4 = (bf16[1,512,128]{2,1,0:T(8,128)(2,1)}, bf16[1,512,128]{2,1,0:T(8,128)(2,1)S(1)}, u32[]{:S(2)}, u32[]{:S(2)}) collective-permute-start(bf16[1,512,128]{2,1,0:T(8,128)(2,1)} %bitcast.18), channel_id=1, source_target_pairs={{0,65},{1,64},{2,67},{3,66},{4,69},{5,68},{6,71},{7,70},{8,56},{9,... | collective-permute-start | bytes 393224 | tf_op jit(solution)/shard_map/ppermute | solution.py:56
  5.8 2.5 %collective-permute-done.4 = bf16[1,512,128]{2,1,0:T(8,128)(2,1)S(1)} collective-permute-done((bf16[1,512,128]{2,1,0:T(8,128)(2,1)}, bf16[1,512,128]{2,1,0:T(8,128)(2,1)S(1)}, u32[]{:S(2)}, u32[]{:S(2)}) %collective-permute-start.4) | collective-permute-done | bytes 131104 | tf_op jit(solution)/shard_map/ppermute | solution.py:56
  8.3 2.2 %collective-permute-done.3 = bf16[1,512,128]{2,1,0:T(8,128)(2,1)S(1)} collective-permute-done((bf16[1,512,128]{2,1,0:T(8,128)(2,1)}, bf16[1,512,128]{2,1,0:T(8,128)(2,1)S(1)}, u32[]{:S(2)}, u32[]{:S(2)}) %collective-permute-start.3) | collective-permute-done | bytes 131104 | tf_op jit(solution)/shard_map/ppermute | solution.py:56
  14.7 2.2 %collective-permute-start.9 = (bf16[4,512,128]{2,1,0:T(8,128)(2,1)S(1)}, bf16[4,512,128]{2,1,0:T(8,128)(2,1)S(1)}, u32[]{:S(2)}, u32[]{:S(2)}) collective-permute-start(bf16[4,512,128]{2,1,0:T(8,128)(2,1)S(1)} %pad_maximum_fusion.1.rest_0_), channel_id=1, source_target_pairs={{0,6},{1,7},{2,0},{3,1},{4,2},{5,3},{6,4},{7,5},{8,14},{9,15},{10,... | collective-permute-start | bytes 1572872 | tf_op jit(solution)/shard_map/ppermute | solution.py:56
  16.9 10.7 %collective-permute-done.8 = bf16[4,512,128]{2,1,0:T(8,128)(2,1)S(1)} collective-permute-done((bf16[4,512,128]{2,1,0:T(8,128)(2,1)S(1)}, bf16[4,512,128]{2,1,0:T(8,128)(2,1)S(1)}, u32[]{:S(2)}, u32[]{:S(2)}) %collective-permute-start.8) | collective-permute-done | bytes 524320 | tf_op jit(solution)/shard_map/ppermute | solution.py:56
  27.8 3.4 %collective-permute-start.12 = (bf16[8,512,128]{2,1,0:T(8,128)(2,1)S(1)}, bf16[8,512,128]{2,1,0:T(8,128)(2,1)}, u32[]{:S(2)}, u32[]{:S(2)}) collective-permute-start(bf16[8,512,128]{2,1,0:T(8,128)(2,1)S(1)} %constant_dynamic-update-slice_fusion.rest_4_), channel_id=1, source_target_pairs={{0,48},{1,49},{2,50},{3,51},{4,52},{5,53},{6,54},{7,55},{8,73},{9,... | collective-permute-start | bytes 3145736 | tf_op jit(solution)/shard_map/ppermute | solution.py:56
  31.1 3.3 %collective-permute-start.10 = (bf16[4,512,128]{2,1,0:T(8,128)(2,1)S(1)}, bf16[4,512,128]{2,1,0:T(8,128)(2,1)S(1)}, u32[]{:S(2)}, u32[]{:S(2)}) collective-permute-start(bf16[4,512,128]{2,1,0:T(8,128)(2,1)S(1)} %pad_maximum_fusion.1.rest_0_), channel_id=1, source_target_pairs={{0,4},{1,5},{2,6},{3,7},{4,0},{5,1},{6,2},{7,3},{8,12},{9,13},{10,... | collective-permute-start | bytes 1572872 | tf_op jit(solution)/shard_map/ppermute | solution.py:56
  36.0 2.7 %collective-permute-start.6 = (bf16[4,512,128]{2,1,0:T(8,128)(2,1)S(1)}, bf16[4,512,128]{2,1,0:T(8,128)(2,1)S(1)}, u32[]{:S(2)}, u32[]{:S(2)}) collective-permute-start(bf16[4,512,128]{2,1,0:T(8,128)(2,1)S(1)} %pad_maximum_fusion.1.rest_0_), channel_id=1, source_target_pairs={{0,48},{1,49},{2,50},{3,51},{4,52},{5,53},{6,54},{7,55},{8,73},{9,... | collective-permute-start | bytes 1572872 | tf_op jit(solution)/shard_map/ppermute | solution.py:56
  38.6 7.1 %collective-permute-done.10.rest_5_ = bf16[4,512,128]{2,1,0:T(8,128)(2,1)S(1)} collective-permute-done((bf16[4,512,128]{2,1,0:T(8,128)(2,1)S(1)}, bf16[4,512,128]{2,1,0:T(8,128)(2,1)S(1)}, u32[]{:S(2)}, u32[]{:S(2)}) %collective-permute-start.10) | collective-permute-done | bytes 524320 | tf_op jit(solution)/shard_map/ppermute | solution.py:56
  45.8 2.7 %collective-permute-done.6.rest_2_ = bf16[4,512,128]{2,1,0:T(8,128)(2,1)S(1)} collective-permute-done((bf16[4,512,128]{2,1,0:T(8,128)(2,1)S(1)}, bf16[4,512,128]{2,1,0:T(8,128)(2,1)S(1)}, u32[]{:S(2)}, u32[]{:S(2)}) %collective-permute-start.6) | collective-permute-done | bytes 524320 | tf_op jit(solution)/shard_map/ppermute | solution.py:56
  50.1 2.4 %collective-permute-start.15 = (bf16[8,512,128]{2,1,0:T(8,128)(2,1)}, bf16[8,512,128]{2,1,0:T(8,128)(2,1)S(1)}, u32[]{:S(2)}, u32[]{:S(2)}) collective-permute-start(bf16[8,512,128]{2,1,0:T(8,128)(2,1)} %collective-permute-done.12.rest_1_), channel_id=1, source_target_pairs={{0,48},{1,49},{2,50},{3,51},{4,52},{5,53},{6,54},{7,55},{8,73},{9,... | collective-permute-start | bytes 3145736 | tf_op jit(solution)/shard_map/ppermute | solution.py:56
  52.4 3.0 %collective-permute-done.13.rest_0_ = bf16[4,512,128]{2,1,0:T(8,128)(2,1)} collective-permute-done((bf16[4,512,128]{2,1,0:T(8,128)(2,1)S(1)}, bf16[4,512,128]{2,1,0:T(8,128)(2,1)}, u32[]{:S(2)}, u32[]{:S(2)}) %collective-permute-start.13) | collective-permute-done | bytes 524320 | tf_op jit(solution)/shard_map/ppermute | solution.py:56
  55.4 5.6 %collective-permute-done.7.rest_3_ = bf16[4,512,128]{2,1,0:T(8,128)(2,1)} collective-permute-done((bf16[4,512,128]{2,1,0:T(8,128)(2,1)}, bf16[4,512,128]{2,1,0:T(8,128)(2,1)}, u32[]{:S(2)}, u32[]{:S(2)}) %collective-permute-start.7) | collective-permute-done | bytes 524320 | tf_op jit(solution)/shard_map/ppermute | solution.py:56
  61.1 12.3 %early_sum.2 = (f32[512,128]{1,0:T(8,128)S(1)}, s32[64]{0:T(128)S(1)}, s32[8]{0:T(128)S(1)}, s32[40]{0:T(128)S(1)}, s32[8]{0:T(128)S(1)}, /*index=5*/s32[48]{0:T(128)S(1)}, s32[8]{0:T(128)S(1)}, f32[8,128]{1,0:T(8,128)S(1)}) custom-call(s32[128]{0:T(128)S(1)} %get-tuple-element.45.order, s32[128]{0:T(128)S(1)} %get-tuple-element.40.skip, ...), custom_call_target="tpu_custom_call" | custom-call | flops 1207959552 | bytes 14155776 | tf_op jit(solution)/shard_map/early_sum/pallas_call | solution.py:380
  73.4 6.0 %shard_map.131.acc_in = f32[1024,128]{1,0:T(8,128)S(1)} custom-call(s32[64]{0:T(128)S(1)} %get-tuple-element.25.codes, s32[8]{0:T(128)S(1)} %get-tuple-element.26.off, f32[512,128]{1,0:T(8,128)S(1)} %get-tuple-element.27.acc_in, bf16[128,256,256]{2,1,0:T(8,128)(2,1)} %bitcast.24, bf16[128,256,256]{2,1,0:T(8,128)(2,1)} %collective-permute-done.1.other, ...), custom_call_target="tpu_custom_call" | custom-call | flops 469762048 | bytes 5505024 | tf_op jit(solution)/shard_map/pallas_call | solution.py:408
  79.5 4.5 %shard_map.132.acc_in = f32[1024,128]{1,0:T(8,128)S(1)} custom-call(s32[40]{0:T(128)S(1)} %get-tuple-element.23.codes, s32[8]{0:T(128)S(1)} %get-tuple-element.24.off, f32[1024,128]{1,0:T(8,128)S(1)} %shard_map.131.acc_in, bf16[128,256,256]{2,1,0:T(8,128)(2,1)} %bitcast.25, bf16[128,256,256]{2,1,0:T(8,128)(2,1)} %collective-permute-done.1.other, ...), custom_call_target="tpu_custom_call" | custom-call | flops 268435456 | bytes 3145728 | tf_op jit(solution)/shard_map/pallas_call | solution.py:408
  84.0 5.1 %late_sum.2 = (f32[512,128]{1,0:T(8,128)S(1)}, f32[512,128]{1,0:T(8,128)S(1)}) custom-call(s32[48]{0:T(128)S(1)} %get-tuple-element.21.codes, s32[8]{0:T(128)S(1)} %get-tuple-element.22.off, s32[64]{0:T(128)S(1)} %fusion.8.jtab, f32[1024,128]{1,0:T(8,128)S(1)} %shard_map.132.acc_in, bf16[128,256,256]{2,1,0:T(8,128)(2,1)} %bitcast.26, ...), custom_call_target="tpu_custom_call" | custom-call | flops 335544320 | bytes 3932160 | tf_op jit(solution)/shard_map/late_sum/pallas_call | solution.py:423
  91.7 2.5 %collective-permute-start.20 = (bf16[1,528,128]{2,1,0:T(8,128)(2,1)S(1)}, bf16[1,528,128]{2,1,0:T(8,128)(2,1)S(1)}, u32[]{:S(2)}, u32[]{:S(2)}) collective-permute-start(bf16[1,528,128]{2,1,0:T(8,128)(2,1)S(1)} %bitcast.14), channel_id=1, source_target_pairs={{0,65},{1,64},{2,67},{3,66},{4,69},{5,68},{6,71},{7,70},{8,56},{9,... | collective-permute-start | bytes 405512 | tf_op jit(solution)/shard_map/ppermute | solution.py:56
  94.9 2.7 %collective-permute-done.20 = bf16[1,528,128]{2,1,0:T(8,128)(2,1)S(1)} collective-permute-done((bf16[1,528,128]{2,1,0:T(8,128)(2,1)S(1)}, bf16[1,528,128]{2,1,0:T(8,128)(2,1)S(1)}, u32[]{:S(2)}, u32[]{:S(2)}) %collective-permute-start.20) | collective-permute-done | bytes 135200 | tf_op jit(solution)/shard_map/ppermute | solution.py:56
  97.7 2.3 %collective-permute-done.19 = bf16[1,528,128]{2,1,0:T(8,128)(2,1)S(1)} collective-permute-done((bf16[1,528,128]{2,1,0:T(8,128)(2,1)S(1)}, bf16[1,528,128]{2,1,0:T(8,128)(2,1)S(1)}, u32[]{:S(2)}, u32[]{:S(2)}) %collective-permute-start.19) | collective-permute-done | bytes 135200 | tf_op jit(solution)/shard_map/ppermute | solution.py:56
  101.8 2.4 %collective-permute-start.25 = (bf16[4,528,128]{2,1,0:T(8,128)(2,1)S(1)}, bf16[4,528,128]{2,1,0:T(8,128)(2,1)S(1)}, u32[]{:S(2)}, u32[]{:S(2)}) collective-permute-start(bf16[4,528,128]{2,1,0:T(8,128)(2,1)S(1)} %pad_maximum_fusion.rest_0_), channel_id=1, source_target_pairs={{0,6},{1,7},{2,0},{3,1},{4,2},{5,3},{6,4},{7,5},{8,14},{9,15},{10,... | collective-permute-start | bytes 1622024 | tf_op jit(solution)/shard_map/ppermute | solution.py:56
  104.2 10.3 %collective-permute-done.24 = bf16[4,528,128]{2,1,0:T(8,128)(2,1)S(1)} collective-permute-done((bf16[4,528,128]{2,1,0:T(8,128)(2,1)S(1)}, bf16[4,528,128]{2,1,0:T(8,128)(2,1)S(1)}, u32[]{:S(2)}, u32[]{:S(2)}) %collective-permute-start.24) | collective-permute-done | bytes 540704 | tf_op jit(solution)/shard_map/ppermute | solution.py:56
  114.6 3.8 %collective-permute-start.28 = (bf16[8,528,128]{2,1,0:T(8,128)(2,1)S(1)}, bf16[8,528,128]{2,1,0:T(8,128)(2,1)S(1)}, u32[]{:S(2)}, u32[]{:S(2)}) collective-permute-start(bf16[8,528,128]{2,1,0:T(8,128)(2,1)S(1)} %constant_dynamic-update-slice_fusion.2.rest_4_), channel_id=1, source_target_pairs={{0,48},{1,49},{2,50},{3,51},{4,52},{5,53},{6,54},{7,55},{8,73},{9,... | collective-permute-start | bytes 3244040 | tf_op jit(solution)/shard_map/ppermute | solution.py:56
  120.5 2.4 %collective-permute-start.22 = (bf16[4,528,128]{2,1,0:T(8,128)(2,1)S(1)}, bf16[4,528,128]{2,1,0:T(8,128)(2,1)S(1)}, u32[]{:S(2)}, u32[]{:S(2)}) collective-permute-start(bf16[4,528,128]{2,1,0:T(8,128)(2,1)S(1)} %pad_maximum_fusion.rest_0_), channel_id=1, source_target_pairs={{0,48},{1,49},{2,50},{3,51},{4,52},{5,53},{6,54},{7,55},{8,73},{9,... | collective-permute-start | bytes 1622024 | tf_op jit(solution)/shard_map/ppermute | solution.py:56
  122.9 11.1 %collective-permute-done.26.rest_5_ = bf16[4,528,128]{2,1,0:T(8,128)(2,1)S(1)} collective-permute-done((bf16[4,528,128]{2,1,0:T(8,128)(2,1)S(1)}, bf16[4,528,128]{2,1,0:T(8,128)(2,1)S(1)}, u32[]{:S(2)}, u32[]{:S(2)}) %collective-permute-start.26) | collective-permute-done | bytes 540704 | tf_op jit(solution)/shard_map/ppermute | solution.py:56
  134.0 2.7 %collective-permute-start.31 = (bf16[8,528,128]{2,1,0:T(8,128)(2,1)S(1)}, bf16[8,528,128]{2,1,0:T(8,128)(2,1)S(1)}, u32[]{:S(2)}, u32[]{:S(2)}) collective-permute-start(bf16[8,528,128]{2,1,0:T(8,128)(2,1)S(1)} %collective-permute-done.28.rest_1_.rest_7_), channel_id=1, source_target_pairs={{0,48},{1,49},{2,50},{3,51},{4,52},{5,53},{6,54},{7,55},{8,73},{9,... | collective-permute-start | bytes 3244040 | tf_op jit(solution)/shard_map/ppermute | solution.py:56
  136.7 3.1 %collective-permute-start.30 = (bf16[4,528,128]{2,1,0:T(8,128)(2,1)S(1)}, bf16[4,528,128]{2,1,0:T(8,128)(2,1)S(1)}, u32[]{:S(2)}, u32[]{:S(2)}) collective-permute-start(bf16[4,528,128]{2,1,0:T(8,128)(2,1)S(1)} %collective-permute-done.26.rest_5_), channel_id=1, source_target_pairs={{0,48},{1,49},{2,50},{3,51},{4,52},{5,53},{6,54},{7,55},{8,73},{9,... | collective-permute-start | bytes 1622024 | tf_op jit(solution)/shard_map/ppermute | solution.py:56
  139.8 7.5 %collective-permute-done.29.rest_8_ = bf16[4,528,128]{2,1,0:T(8,128)(2,1)S(1)} collective-permute-done((bf16[4,528,128]{2,1,0:T(8,128)(2,1)S(1)}, bf16[4,528,128]{2,1,0:T(8,128)(2,1)S(1)}, u32[]{:S(2)}, u32[]{:S(2)}) %collective-permute-start.29) | collective-permute-done | bytes 540704 | tf_op jit(solution)/shard_map/ppermute | solution.py:56
  147.3 11.9 %early_sum.3 = (f32[512,128]{1,0:T(8,128)S(1)}, s32[64]{0:T(128)S(1)}, s32[8]{0:T(128)S(1)}, s32[40]{0:T(128)S(1)}, s32[8]{0:T(128)S(1)}, /*index=5*/s32[48]{0:T(128)S(1)}, s32[8]{0:T(128)S(1)}, f32[8,128]{1,0:T(8,128)}) custom-call(s32[128]{0:T(128)S(1)} %get-tuple-element.44.order, s32[128]{0:T(128)S(1)} %get-tuple-element.41.skip, ...), custom_call_target="tpu_custom_call" | custom-call | flops 1207959552 | bytes 14155776 | tf_op jit(solution)/shard_map/early_sum/pallas_call | solution.py:380
  159.2 4.6 %shard_map.133.acc_in = f32[1024,128]{1,0:T(8,128)S(1)} custom-call(s32[64]{0:T(128)S(1)} %get-tuple-element.35.codes, s32[8]{0:T(128)S(1)} %get-tuple-element.36.off, f32[512,128]{1,0:T(8,128)S(1)} %get-tuple-element.37.acc_in, bf16[128,256,256]{2,1,0:T(8,128)(2,1)} %bitcast.28, bf16[128,256,256]{2,1,0:T(8,128)(2,1)} %collective-permute-done.1.other, ...), custom_call_target="tpu_custom_call" | custom-call | flops 469762048 | bytes 5505024 | tf_op jit(solution)/shard_map/pallas_call | solution.py:408
  163.8 4.6 %shard_map.134.acc_in = f32[1024,128]{1,0:T(8,128)S(1)} custom-call(s32[40]{0:T(128)S(1)} %get-tuple-element.33.codes, s32[8]{0:T(128)S(1)} %get-tuple-element.34.off, f32[1024,128]{1,0:T(8,128)S(1)} %shard_map.133.acc_in, bf16[128,256,256]{2,1,0:T(8,128)(2,1)} %bitcast.29, bf16[128,256,256]{2,1,0:T(8,128)(2,1)} %collective-permute-done.1.other, ...), custom_call_target="tpu_custom_call" | custom-call | flops 268435456 | bytes 3145728 | tf_op jit(solution)/shard_map/pallas_call | solution.py:408
  168.5 4.4 %late_sum.3 = (f32[528,128]{1,0:T(8,128)S(1)}, f32[528,128]{1,0:T(8,128)S(1)}) custom-call(s32[48]{0:T(128)S(1)} %get-tuple-element.31.codes, s32[8]{0:T(128)S(1)} %get-tuple-element.32.off, s32[64]{0:T(128)S(1)} %fusion.8.jtab, f32[1024,128]{1,0:T(8,128)S(1)} %shard_map.134.acc_in, bf16[128,256,256]{2,1,0:T(8,128)(2,1)} %bitcast.30, ...), custom_call_target="tpu_custom_call" | custom-call | flops 335544320 | bytes 3932160 | tf_op jit(solution)/shard_map/late_sum/pallas_call | solution.py:423
  (78 shorter events, 21.1 us)
Async XLA Ops:
  0.6 72.8 %collective-permute-start.1 = (bf16[128,256,256]{2,1,0:T(8,128)(2,1)}, bf16[128,256,256]{2,1,0:T(8,128)(2,1)}, u32[]{:S(2)}, u32[]{:S(2)}) collective-permute-start(bf16[128,256,256]{2,1,0:T(8,128)(2,1)} %bitcast.22), channel_id=1, source_target_pairs={{0,8},{1,9},{2,10},{3,11},{4,12},{5,13},{6,14},{7,15},{8,0},{9,1},... | collective-permute-start | bytes 50331656 | tf_op jit(solution)/shard_map/ppermute | solution.py:60
  2.1 6.3 %collective-permute-start.4 = (bf16[1,512,128]{2,1,0:T(8,128)(2,1)}, bf16[1,512,128]{2,1,0:T(8,128)(2,1)S(1)}, u32[]{:S(2)}, u32[]{:S(2)}) collective-permute-start(bf16[1,512,128]{2,1,0:T(8,128)(2,1)} %bitcast.18), channel_id=1, source_target_pairs={{0,65},{1,64},{2,67},{3,66},{4,69},{5,68},{6,71},{7,70},{8,56},{9,... | collective-permute-start | bytes 393224 | tf_op jit(solution)/shard_map/ppermute | solution.py:56
  4.7 5.8 %collective-permute-start.3 = (bf16[1,512,128]{2,1,0:T(8,128)(2,1)}, bf16[1,512,128]{2,1,0:T(8,128)(2,1)S(1)}, u32[]{:S(2)}, u32[]{:S(2)}) collective-permute-start(bf16[1,512,128]{2,1,0:T(8,128)(2,1)} %bitcast.19), channel_id=1, source_target_pairs={{0,1},{1,0},{2,3},{3,2},{4,5},{5,4},{6,7},{7,6},{8,40},{9,41},{10,... | collective-permute-start | bytes 393224 | tf_op jit(solution)/shard_map/ppermute | solution.py:56
  5.2 6.7 %collective-permute-start.2 = (bf16[1,512,128]{2,1,0:T(8,128)(2,1)}, bf16[1,512,128]{2,1,0:T(8,128)(2,1)S(1)}, u32[]{:S(2)}, u32[]{:S(2)}) collective-permute-start(bf16[1,512,128]{2,1,0:T(8,128)(2,1)} %bitcast.20), channel_id=1, source_target_pairs={{0,64},{1,65},{2,66},{3,67},{4,68},{5,69},{6,70},{7,71},{8,24},{9,... | collective-permute-start | bytes 393224 | tf_op jit(solution)/shard_map/ppermute | solution.py:56
  13.0 14.7 %collective-permute-start.8 = (bf16[4,512,128]{2,1,0:T(8,128)(2,1)S(1)}, bf16[4,512,128]{2,1,0:T(8,128)(2,1)S(1)}, u32[]{:S(2)}, u32[]{:S(2)}) collective-permute-start(bf16[4,512,128]{2,1,0:T(8,128)(2,1)S(1)} %pad_maximum_fusion.1.rest_0_), channel_id=1, source_target_pairs={{0,2},{1,3},{2,4},{3,5},{4,6},{5,7},{6,0},{7,1},{8,10},{9,11},{10,... | collective-permute-start | bytes 1572872 | tf_op jit(solution)/shard_map/ppermute | solution.py:56
  14.7 13.0 %collective-permute-start.9 = (bf16[4,512,128]{2,1,0:T(8,128)(2,1)S(1)}, bf16[4,512,128]{2,1,0:T(8,128)(2,1)S(1)}, u32[]{:S(2)}, u32[]{:S(2)}) collective-permute-start(bf16[4,512,128]{2,1,0:T(8,128)(2,1)S(1)} %pad_maximum_fusion.1.rest_0_), channel_id=1, source_target_pairs={{0,6},{1,7},{2,0},{3,1},{4,2},{5,3},{6,4},{7,5},{8,14},{9,15},{10,... | collective-permute-start | bytes 1572872 | tf_op jit(solution)/shard_map/ppermute | solution.py:56
  27.8 22.3 %collective-permute-start.12 = (bf16[8,512,128]{2,1,0:T(8,128)(2,1)S(1)}, bf16[8,512,128]{2,1,0:T(8,128)(2,1)}, u32[]{:S(2)}, u32[]{:S(2)}) collective-permute-start(bf16[8,512,128]{2,1,0:T(8,128)(2,1)S(1)} %constant_dynamic-update-slice_fusion.rest_4_), channel_id=1, source_target_pairs={{0,48},{1,49},{2,50},{3,51},{4,52},{5,53},{6,54},{7,55},{8,73},{9,... | collective-permute-start | bytes 3145736 | tf_op jit(solution)/shard_map/ppermute | solution.py:56
  31.1 14.6 %collective-permute-start.10 = (bf16[4,512,128]{2,1,0:T(8,128)(2,1)S(1)}, bf16[4,512,128]{2,1,0:T(8,128)(2,1)S(1)}, u32[]{:S(2)}, u32[]{:S(2)}) collective-permute-start(bf16[4,512,128]{2,1,0:T(8,128)(2,1)S(1)} %pad_maximum_fusion.1.rest_0_), channel_id=1, source_target_pairs={{0,4},{1,5},{2,6},{3,7},{4,0},{5,1},{6,2},{7,3},{8,12},{9,13},{10,... | collective-permute-start | bytes 1572872 | tf_op jit(solution)/shard_map/ppermute | solution.py:56
  34.4 11.3 %collective-permute-start.5 = (bf16[4,512,128]{2,1,0:T(8,128)(2,1)S(1)}, bf16[4,512,128]{2,1,0:T(8,128)(2,1)}, u32[]{:S(2)}, u32[]{:S(2)}) collective-permute-start(bf16[4,512,128]{2,1,0:T(8,128)(2,1)S(1)} %pad_maximum_fusion.1.rest_0_), channel_id=1, source_target_pairs={{0,16},{1,17},{2,18},{3,19},{4,20},{5,21},{6,22},{7,23},{8,72},{9,... | collective-permute-start | bytes 1572872 | tf_op jit(solution)/shard_map/ppermute | solution.py:56
  36.0 12.6 %collective-permute-start.6 = (bf16[4,512,128]{2,1,0:T(8,128)(2,1)S(1)}, bf16[4,512,128]{2,1,0:T(8,128)(2,1)S(1)}, u32[]{:S(2)}, u32[]{:S(2)}) collective-permute-start(bf16[4,512,128]{2,1,0:T(8,128)(2,1)S(1)} %pad_maximum_fusion.1.rest_0_), channel_id=1, source_target_pairs={{0,48},{1,49},{2,50},{3,51},{4,52},{5,53},{6,54},{7,55},{8,73},{9,... | collective-permute-start | bytes 1572872 | tf_op jit(solution)/shard_map/ppermute | solution.py:56
  45.8 9.6 %collective-permute-start.13 = (bf16[4,512,128]{2,1,0:T(8,128)(2,1)S(1)}, bf16[4,512,128]{2,1,0:T(8,128)(2,1)}, u32[]{:S(2)}, u32[]{:S(2)}) collective-permute-start(bf16[4,512,128]{2,1,0:T(8,128)(2,1)S(1)} %collective-permute-done.10.rest_5_), channel_id=1, source_target_pairs={{0,16},{1,17},{2,18},{3,19},{4,20},{5,21},{6,22},{7,23},{8,72},{9,... | collective-permute-start | bytes 1572872 | tf_op jit(solution)/shard_map/ppermute | solution.py:56
  45.8 15.3 %collective-permute-start.7 = (bf16[4,512,128]{2,1,0:T(8,128)(2,1)}, bf16[4,512,128]{2,1,0:T(8,128)(2,1)}, u32[]{:S(2)}, u32[]{:S(2)}) collective-permute-start(bf16[4,512,128]{2,1,0:T(8,128)(2,1)} %collective-permute-done.5.rest_1_), channel_id=1, source_target_pairs={{0,16},{1,17},{2,18},{3,19},{4,20},{5,21},{6,22},{7,23},{8,72},{9,... | collective-permute-start | bytes 1572872 | tf_op jit(solution)/shard_map/ppermute | solution.py:56
  49.3 30.2 %collective-permute-start.11 = (bf16[8,512,128]{2,1,0:T(8,128)(2,1)S(1)}, bf16[8,512,128]{2,1,0:T(8,128)(2,1)}, u32[]{:S(2)}, u32[]{:S(2)}) collective-permute-start(bf16[8,512,128]{2,1,0:T(8,128)(2,1)S(1)} %constant_dynamic-update-slice_fusion.rest_4_), channel_id=1, source_target_pairs={{0,16},{1,17},{2,18},{3,19},{4,20},{5,21},{6,22},{7,23},{8,72},{9,... | collective-permute-start | bytes 3145736 | tf_op jit(solution)/shard_map/ppermute | solution.py:56
  50.1 33.9 %collective-permute-start.15 = (bf16[8,512,128]{2,1,0:T(8,128)(2,1)}, bf16[8,512,128]{2,1,0:T(8,128)(2,1)S(1)}, u32[]{:S(2)}, u32[]{:S(2)}) collective-permute-start(bf16[8,512,128]{2,1,0:T(8,128)(2,1)} %collective-permute-done.12.rest_1_), channel_id=1, source_target_pairs={{0,48},{1,49},{2,50},{3,51},{4,52},{5,53},{6,54},{7,55},{8,73},{9,... | collective-permute-start | bytes 3145736 | tf_op jit(solution)/shard_map/ppermute | solution.py:56
  55.4 28.6 %collective-permute-start.14 = (bf16[4,512,128]{2,1,0:T(8,128)(2,1)S(1)}, bf16[4,512,128]{2,1,0:T(8,128)(2,1)S(1)}, u32[]{:S(2)}, u32[]{:S(2)}) collective-permute-start(bf16[4,512,128]{2,1,0:T(8,128)(2,1)S(1)} %collective-permute-done.10.rest_5_), channel_id=1, source_target_pairs={{0,48},{1,49},{2,50},{3,51},{4,52},{5,53},{6,54},{7,55},{8,73},{9,... | collective-permute-start | bytes 1572872 | tf_op jit(solution)/shard_map/ppermute | solution.py:56
  61.0 23.0 %collective-permute-start.16 = (bf16[4,512,128]{2,1,0:T(8,128)(2,1)}, bf16[4,512,128]{2,1,0:T(8,128)(2,1)S(1)}, u32[]{:S(2)}, u32[]{:S(2)}) collective-permute-start(bf16[4,512,128]{2,1,0:T(8,128)(2,1)} %collective-permute-done.13.rest_0_), channel_id=1, source_target_pairs={{0,16},{1,17},{2,18},{3,19},{4,20},{5,21},{6,22},{7,23},{8,72},{9,... | collective-permute-start | bytes 1572872 | tf_op jit(solution)/shard_map/ppermute | solution.py:56
  91.7 5.9 %collective-permute-start.20 = (bf16[1,528,128]{2,1,0:T(8,128)(2,1)S(1)}, bf16[1,528,128]{2,1,0:T(8,128)(2,1)S(1)}, u32[]{:S(2)}, u32[]{:S(2)}) collective-permute-start(bf16[1,528,128]{2,1,0:T(8,128)(2,1)S(1)} %bitcast.14), channel_id=1, source_target_pairs={{0,65},{1,64},{2,67},{3,66},{4,69},{5,68},{6,71},{7,70},{8,56},{9,... | collective-permute-start | bytes 405512 | tf_op jit(solution)/shard_map/ppermute | solution.py:56
  94.2 5.7 %collective-permute-start.19 = (bf16[1,528,128]{2,1,0:T(8,128)(2,1)S(1)}, bf16[1,528,128]{2,1,0:T(8,128)(2,1)S(1)}, u32[]{:S(2)}, u32[]{:S(2)}) collective-permute-start(bf16[1,528,128]{2,1,0:T(8,128)(2,1)S(1)} %bitcast.15), channel_id=1, source_target_pairs={{0,1},{1,0},{2,3},{3,2},{4,5},{5,4},{6,7},{7,6},{8,40},{9,41},{10,... | collective-permute-start | bytes 405512 | tf_op jit(solution)/shard_map/ppermute | solution.py:56
  94.3 6.8 %collective-permute-start.18 = (bf16[1,528,128]{2,1,0:T(8,128)(2,1)S(1)}, bf16[1,528,128]{2,1,0:T(8,128)(2,1)S(1)}, u32[]{:S(2)}, u32[]{:S(2)}) collective-permute-start(bf16[1,528,128]{2,1,0:T(8,128)(2,1)S(1)} %bitcast.16), channel_id=1, source_target_pairs={{0,64},{1,65},{2,66},{3,67},{4,68},{5,69},{6,70},{7,71},{8,24},{9,... | collective-permute-start | bytes 405512 | tf_op jit(solution)/shard_map/ppermute | solution.py:56
  101.1 13.4 %collective-permute-start.24 = (bf16[4,528,128]{2,1,0:T(8,128)(2,1)S(1)}, bf16[4,528,128]{2,1,0:T(8,128)(2,1)S(1)}, u32[]{:S(2)}, u32[]{:S(2)}) collective-permute-start(bf16[4,528,128]{2,1,0:T(8,128)(2,1)S(1)} %pad_maximum_fusion.rest_0_), channel_id=1, source_target_pairs={{0,2},{1,3},{2,4},{3,5},{4,6},{5,7},{6,0},{7,1},{8,10},{9,11},{10,... | collective-permute-start | bytes 1622024 | tf_op jit(solution)/shard_map/ppermute | solution.py:56
  101.8 12.8 %collective-permute-start.25 = (bf16[4,528,128]{2,1,0:T(8,128)(2,1)S(1)}, bf16[4,528,128]{2,1,0:T(8,128)(2,1)S(1)}, u32[]{:S(2)}, u32[]{:S(2)}) collective-permute-start(bf16[4,528,128]{2,1,0:T(8,128)(2,1)S(1)} %pad_maximum_fusion.rest_0_), channel_id=1, source_target_pairs={{0,6},{1,7},{2,0},{3,1},{4,2},{5,3},{6,4},{7,5},{8,14},{9,15},{10,... | collective-permute-start | bytes 1622024 | tf_op jit(solution)/shard_map/ppermute | solution.py:56
  114.6 19.4 %collective-permute-start.28 = (bf16[8,528,128]{2,1,0:T(8,128)(2,1)S(1)}, bf16[8,528,128]{2,1,0:T(8,128)(2,1)S(1)}, u32[]{:S(2)}, u32[]{:S(2)}) collective-permute-start(bf16[8,528,128]{2,1,0:T(8,128)(2,1)S(1)} %constant_dynamic-update-slice_fusion.2.rest_4_), channel_id=1, source_target_pairs={{0,48},{1,49},{2,50},{3,51},{4,52},{5,53},{6,54},{7,55},{8,73},{9,... | collective-permute-start | bytes 3244040 | tf_op jit(solution)/shard_map/ppermute | solution.py:56
  118.5 15.5 %collective-permute-start.26 = (bf16[4,528,128]{2,1,0:T(8,128)(2,1)S(1)}, bf16[4,528,128]{2,1,0:T(8,128)(2,1)S(1)}, u32[]{:S(2)}, u32[]{:S(2)}) collective-permute-start(bf16[4,528,128]{2,1,0:T(8,128)(2,1)S(1)} %pad_maximum_fusion.rest_0_), channel_id=1, source_target_pairs={{0,4},{1,5},{2,6},{3,7},{4,0},{5,1},{6,2},{7,3},{8,12},{9,13},{10,... | collective-permute-start | bytes 1622024 | tf_op jit(solution)/shard_map/ppermute | solution.py:56
  120.2 16.5 %collective-permute-start.21 = (bf16[4,528,128]{2,1,0:T(8,128)(2,1)S(1)}, bf16[4,528,128]{2,1,0:T(8,128)(2,1)S(1)}, u32[]{:S(2)}, u32[]{:S(2)}) collective-permute-start(bf16[4,528,128]{2,1,0:T(8,128)(2,1)S(1)} %pad_maximum_fusion.rest_0_), channel_id=1, source_target_pairs={{0,16},{1,17},{2,18},{3,19},{4,20},{5,21},{6,22},{7,23},{8,72},{9,... | collective-permute-start | bytes 1622024 | tf_op jit(solution)/shard_map/ppermute | solution.py:56
  120.2 43.7 %collective-permute-start.27 = (bf16[8,528,128]{2,1,0:T(8,128)(2,1)S(1)}, bf16[8,528,128]{2,1,0:T(8,128)(2,1)S(1)}, u32[]{:S(2)}, u32[]{:S(2)}) collective-permute-start(bf16[8,528,128]{2,1,0:T(8,128)(2,1)S(1)} %constant_dynamic-update-slice_fusion.2.rest_4_), channel_id=1, source_target_pairs={{0,16},{1,17},{2,18},{3,19},{4,20},{5,21},{6,22},{7,23},{8,72},{9,... | collective-permute-start | bytes 3244040 | tf_op jit(solution)/shard_map/ppermute | solution.py:56
  120.5 16.2 %collective-permute-start.22 = (bf16[4,528,128]{2,1,0:T(8,128)(2,1)S(1)}, bf16[4,528,128]{2,1,0:T(8,128)(2,1)S(1)}, u32[]{:S(2)}, u32[]{:S(2)}) collective-permute-start(bf16[4,528,128]{2,1,0:T(8,128)(2,1)S(1)} %pad_maximum_fusion.rest_0_), channel_id=1, source_target_pairs={{0,48},{1,49},{2,50},{3,51},{4,52},{5,53},{6,54},{7,55},{8,73},{9,... | collective-permute-start | bytes 1622024 | tf_op jit(solution)/shard_map/ppermute | solution.py:56
  134.0 13.3 %collective-permute-start.29 = (bf16[4,528,128]{2,1,0:T(8,128)(2,1)S(1)}, bf16[4,528,128]{2,1,0:T(8,128)(2,1)S(1)}, u32[]{:S(2)}, u32[]{:S(2)}) collective-permute-start(bf16[4,528,128]{2,1,0:T(8,128)(2,1)S(1)} %collective-permute-done.26.rest_5_), channel_id=1, source_target_pairs={{0,16},{1,17},{2,18},{3,19},{4,20},{5,21},{6,22},{7,23},{8,72},{9,... | collective-permute-start | bytes 1622024 | tf_op jit(solution)/shard_map/ppermute | solution.py:56
  134.0 34.5 %collective-permute-start.31 = (bf16[8,528,128]{2,1,0:T(8,128)(2,1)S(1)}, bf16[8,528,128]{2,1,0:T(8,128)(2,1)S(1)}, u32[]{:S(2)}, u32[]{:S(2)}) collective-permute-start(bf16[8,528,128]{2,1,0:T(8,128)(2,1)S(1)} %collective-permute-done.28.rest_1_.rest_7_), channel_id=1, source_target_pairs={{0,48},{1,49},{2,50},{3,51},{4,52},{5,53},{6,54},{7,55},{8,73},{9,... | collective-permute-start | bytes 3244040 | tf_op jit(solution)/shard_map/ppermute | solution.py:56
  136.7 22.5 %collective-permute-start.23 = (bf16[4,528,128]{2,1,0:T(8,128)(2,1)S(1)}, bf16[4,528,128]{2,1,0:T(8,128)(2,1)S(1)}, u32[]{:S(2)}, u32[]{:S(2)}) collective-permute-start(bf16[4,528,128]{2,1,0:T(8,128)(2,1)S(1)} %collective-permute-done.21.rest_1_), channel_id=1, source_target_pairs={{0,16},{1,17},{2,18},{3,19},{4,20},{5,21},{6,22},{7,23},{8,72},{9,... | collective-permute-start | bytes 1622024 | tf_op jit(solution)/shard_map/ppermute | solution.py:56
  136.7 31.8 %collective-permute-start.30 = (bf16[4,528,128]{2,1,0:T(8,128)(2,1)S(1)}, bf16[4,528,128]{2,1,0:T(8,128)(2,1)S(1)}, u32[]{:S(2)}, u32[]{:S(2)}) collective-permute-start(bf16[4,528,128]{2,1,0:T(8,128)(2,1)S(1)} %collective-permute-done.26.rest_5_), channel_id=1, source_target_pairs={{0,48},{1,49},{2,50},{3,51},{4,52},{5,53},{6,54},{7,55},{8,73},{9,... | collective-permute-start | bytes 1622024 | tf_op jit(solution)/shard_map/ppermute | solution.py:56
  147.3 21.2 %collective-permute-start.32 = (bf16[4,528,128]{2,1,0:T(8,128)(2,1)S(1)}, bf16[4,528,128]{2,1,0:T(8,128)(2,1)S(1)}, u32[]{:S(2)}, u32[]{:S(2)}) collective-permute-start(bf16[4,528,128]{2,1,0:T(8,128)(2,1)S(1)} %collective-permute-done.29.rest_8_), channel_id=1, source_target_pairs={{0,16},{1,17},{2,18},{3,19},{4,20},{5,21},{6,22},{7,23},{8,72},{9,... | collective-permute-start | bytes 1622024 | tf_op jit(solution)/shard_map/ppermute | solution.py:56
  172.9 3.0 %collective-permute-start.33 = (f32[528,128]{1,0:T(8,128)S(1)}, f32[528,128]{1,0:T(8,128)S(1)}, u32[]{:S(2)}, u32[]{:S(2)}) collective-permute-start(f32[528,128]{1,0:T(8,128)S(1)} %get-tuple-element.39), channel_id=1, source_target_pairs={{0,8},{1,9},{2,10},{3,11},{4,12},{5,13},{6,14},{7,15},{8,0},{9,1},... | collective-permute-start | bytes 811016 | tf_op jit(solution)/shard_map/ppermute | solution.py:60
  (13 other events, 340.4 us)

commit v2 on v1

--- a/solution.py
+++ b/solution.py
@@ -21,8 +21,8 @@
 QC = [(k, 2) for k in range(4)]
 GROUPS = (
     ((QA, 0), (QA, 1), (QA, 3), (QA, 2), (QB, 0), (QC, 0)),
-    ((QB, 1), (QB, 3)),
-    ((QC, 1), (QC, 3), (QB, 2), (QC, 2)),
+    ((QB, 1), (QB, 3), (QC, 1), (QC, 3)),
+    ((QB[:4], 2), (QB[4:], 2), (QC, 2)),
 )
 
 
@@ -66,15 +66,16 @@
     q1, q3, q2 = (shift(qa, 1, k) for k in (1, 3, 2))
     ap = shift(qa, 2, 1)
     am = shift(qa, 2, 3)
-    fa = shift(ap, 2, 1)
+    ao = shift(qa, 2, 2)
     qb = jnp.concatenate([q1, q3], 0)
     bp = shift(qb, 2, 1)
     bm = shift(qb, 2, 3)
-    fb = shift(bm, 2, 3)
     cp = shift(q2, 2, 1)
     cm = shift(q2, 2, 3)
-    fc = shift(cp, 2, 1)
-    return [qa, ap, am, fa, qb, q2], [bp, bm], [cp, cm, fb, fc]
+    co = shift(q2, 2, 2)
+    fm = shift(bm[:4], 2, 3)
+    fp = shift(bp[4:], 2, 1)
+    return [qa, ap, am, ao, qb, q2], [bp, bm, cp, cm], [fm, fp, co]
 
 
 def item_blocks():
@@ -128,15 +129,21 @@
     pltpu.make_async_copy(tiles.at[0], tbuf.at[slot], tsem.at[slot]).wait()
 
 
+def steps_of(n):
+    return groups_of(n) * UNROLL
+
+
+def prime(n, start, depth):
+    def body(t, c):
+        start(t, t)
+        return c
+
+    lax.fori_loop(0, jnp.minimum(steps_of(n), depth), body, 0)
+
+
 def run(n, start, wait, source, codes, accs, tbuf):
     depth = tbuf.shape[0]
-    total = groups_of(n) * UNROLL
-
-    def prime(t, c):
-        start(t, t)
-        return c
-
-    lax.fori_loop(0, jnp.minimum(total, depth), prime, 0)
+    total = steps_of(n)
 
     def body(g, c):
         first = g * UNROLL
@@ -161,110 +168,119 @@
     lax.fori_loop(0, groups_of(n), body, 0)
 
 
-def run_staged(n, codes, accs, tiles, other, tbuf, tsem, stage):
+def fill_stage(codes, first, last, ref, stage):
+    def body(t, c):
+        code = codes[t]
+        stage[t] = ref[code >> 16, half_rows(code), :]
+        return c
+
+    lax.fori_loop(first, last, body, 0)
+
+
+def total_of(accs, first, rows):
+    total = accs[0, first : first + rows, :]
+    for u in range(1, UNROLL):
+        total = total + accs[u, first : first + rows, :]
+    return total
+
+
+def plan_kernel(order, skip, pos, pos2, jtab, own, *outs):
+    flags = outs[-1]
+    me = own[0]
+    for layer in range(2):
+        clist, nc, *lists = outs[layer * 8 : layer * 8 + 8]
+
+        def set_flag(r, c):
+            flags[order[layer * NB + r]] = 1 - skip[layer * NB + r]
+            return c
+
+        lax.fori_loop(0, NB, set_flag, 0, unroll=8)
+
+        def stale(j, n):
+            clist[n] = (j << 4) | (pos[2 * j + 1] << 3) | pos[2 * j]
+            return n + jnp.where((flags[j] == 0) & (j != me), 1, 0)
+
+        n = lax.fori_loop(0, NB, stale, 0, unroll=8)
+        nc[0] = n
+        pad(clist, n)
+        base = 0
+        for group in range(3):
+            out, off = lists[2 * group], lists[2 * group + 1]
+            n = 0
+            for p, size in enumerate(sizes(group)):
+                off[p] = n
+
+                def build(s, n):
+                    j = jtab[base + s]
+                    fresh = flags[j]
+                    low = (s << 16) | (j << 4)
+                    out[n] = low | (pos[2 * j + 1] << 3) | pos[2 * j]
+                    n = n + jnp.where((fresh == 1) | (j == me), 1, 0)
+                    out[n] = low | (pos2[2 * j + 1] << 3) | 2 | pos2[2 * j]
+                    return n + fresh
+
+                n = lax.fori_loop(0, size, build, n, unroll=4)
+                base += size
+            off[len(sizes(group))] = n
+            pad(out, n)
+
+
+def early_kernel(
+    own, clist, nc, tiles, cached, block, acc, drift, accs, tbuf, sbuf, own_buf, tsem, ssem, osem
+):
+    def source_copy(t, slot):
+        code = clist[t]
+        return pltpu.make_async_copy(
+            cached.at[(code >> 4) & 127, half_rows(code), :], sbuf.at[slot], ssem.at[slot]
+        )
+
+    def tile_copy(t, slot):
+        return pltpu.make_async_copy(
+            tiles.at[(clist[t] >> 4) & 127], tbuf.at[slot], tsem.at[slot]
+        )
+
+    def start(t, slot):
+        tile_copy(t, slot).start()
+        source_copy(t, slot).start()
+
+    def wait(t, slot):
+        tile_copy(t, slot).wait()
+        source_copy(t, slot).wait()
+
+    n = nc[0]
+    prime(n, start, tbuf.shape[0])
+    own_copy = pltpu.make_async_copy(cached.at[own[0]], own_buf, osem)
+    own_copy.start()
+    accs[:, 0:ROWS, :] = jnp.zeros((UNROLL, ROWS, W), jnp.float32)
+    run(n, start, wait, lambda t, slot: sbuf[slot], clist, accs, tbuf)
+    acc[...] = total_of(accs, 0, ROWS)
+    own_copy.wait()
+    diff = block[0:ROWS, :].astype(jnp.float32) - own_buf[...].astype(jnp.float32)
+    drift[...] = jnp.broadcast_to(jnp.sum(diff * diff, axis=0, keepdims=True), (8, W))
+
+
+def add_pieces(
+    codes, off, tiles, other, pieces, accs, tbuf, stage, tsem, then=lambda: None
+):
+    n = off[len(pieces)]
+
+    def start(t, slot):
+        start_tile(tiles, other, tbuf, tsem, codes[t], slot)
+
+    prime(n, start, tbuf.shape[0])
+    then()
+    accs[:, 0 : 2 * ROWS, :] = jnp.zeros((UNROLL, 2 * ROWS, W), jnp.float32)
+    for p, ref in enumerate(pieces):
+        fill_stage(codes, off[p], off[p + 1], ref, stage)
     run(
         n,
-        lambda t, slot: start_tile(tiles, other, tbuf, tsem, codes[t], slot),
+        start,
         lambda t, slot: wait_tile(tiles, tbuf, tsem, slot),
         lambda t, slot: stage[t],
         codes,
         accs,
         tbuf,
     )
-
-
-def fill_stage(codes, first, last, ref, stage):
-    def body(t, c):
-        code = codes[t]
-        stage[t] = ref[code >> 16, half_rows(code), :]
-        return c
-
-    lax.fori_loop(first, last, body, 0)
-
-
-def total_of(accs, first, rows):
-    total = accs[0, first : first + rows, :]
-    for u in range(1, UNROLL):
-        total = total + accs[u, first : first + rows, :]
-    return total
-
-
-def early_kernel(
-    order, skip, pos, pos2, jtab, own, tiles, cached, block,
-    acc, list1, off1, list2, off2, list3, off3, drift,
-    clist, flags, accs, tbuf, sbuf, own_buf, tsem, ssem, osem,
-):
-    me = own[0]
-    own_copy = pltpu.make_async_copy(cached.at[me], own_buf, osem)
-    own_copy.start()
-
-    def set_flag(r, c):
-        flags[order[r]] = 1 - skip[r]
-        return c
-
-    lax.fori_loop(0, NB, set_flag, 0)
-
-    def stale(j, n):
-        clist[n] = (j << 4) | (pos[2 * j + 1] << 3) | pos[2 * j]
-        return n + jnp.where((flags[j] == 0) & (j != me), 1, 0)
-
-    nc = lax.fori_loop(0, NB, stale, 0)
-    pad(clist, nc)
-
-    def split(first, last, n, out):
-        def build(t, n):
-            j = jtab[t]
-            fresh = flags[j]
-            low = ((t - first) << 16) | (j << 4)
-            out[n] = low | (pos[2 * j + 1] << 3) | pos[2 * j]
-            n = n + jnp.where((fresh == 1) | (j == me), 1, 0)
-            out[n] = low | (pos2[2 * j + 1] << 3) | 2 | pos2[2 * j]
-            return n + fresh
-
-        return lax.fori_loop(first, last, build, n)
-
-    base = 0
-    for group, (out, off) in enumerate(((list1, off1), (list2, off2), (list3, off3))):
-        n = 0
-        for p, size in enumerate(sizes(group)):
-            off[p] = n
-            n = split(base, base + size, n, out)
-            base += size
-        off[len(sizes(group))] = n
-        pad(out, n)
-    accs[...] = jnp.zeros_like(accs)
-
-    def source_copy(t, slot):
-        code = clist[t]
-        return pltpu.make_async_copy(
-            cached.at[(code >> 4) & 127, half_rows(code), :], sbuf.at[slot], ssem.at[slot]
-        )
-
-    def tile_copy(t, slot):
-        return pltpu.make_async_copy(
-            tiles.at[(clist[t] >> 4) & 127], tbuf.at[slot], tsem.at[slot]
-        )
-
-    def start(t, slot):
-        tile_copy(t, slot).start()
-        source_copy(t, slot).start()
-
-    def wait(t, slot):
-        tile_copy(t, slot).wait()
-        source_copy(t, slot).wait()
-
-    run(nc, start, wait, lambda t, slot: sbuf[slot], clist, accs, tbuf)
-    acc[...] = total_of(accs, 0, ROWS)
-    own_copy.wait()
-    diff = block[0:ROWS, :].astype(jnp.float32) - own_buf[...].astype(jnp.float32)
-    drift[...] = jnp.broadcast_to(jnp.sum(diff * diff, axis=0, keepdims=True), (8, W))
-
-
-def add_pieces(codes, off, tiles, other, pieces, accs, tbuf, stage, tsem):
-    accs[...] = jnp.zeros_like(accs)
-    for p, ref in enumerate(pieces):
-        fill_stage(codes, off[p], off[p + 1], ref, stage)
-    run_staged(off[len(pieces)], codes, accs, tiles, other, tbuf, tsem, stage)
 
 
 def mid_kernel(codes, off, acc_in, tiles, other, *rest):
@@ -276,15 +292,47 @@
         acc[have:, :] = total_of(accs, have, 2 * ROWS - have)
 
 
-def late_kernel(codes, off, jtab, acc_in, tiles, other, *rest, drifts):
+def mid_fetch_kernel(next_codes, next_off, codes, off, acc_in, tiles, other, *rest):
+    acc, fetched, accs, tbuf, stage, tsem, fsem = rest[-7:]
+    n = steps_of(next_off[len(sizes(2))])
+
+    def start(t, c):
+        start_tile(tiles, other, fetched, fsem, next_codes[t], t)
+        return c
+
+    def wait(t, c):
+        wait_tile(tiles, fetched, fsem, t)
+        return c
+
+    add_pieces(
+        codes, off, tiles, other, rest[:-7], accs, tbuf, stage, tsem,
+        lambda: lax.fori_loop(0, n, start, 0),
+    )
+    acc[...] = acc_in[...] + total_of(accs, 0, 2 * ROWS)
+    lax.fori_loop(0, n, wait, 0)
+
+
+def late_kernel(codes, off, jtab, acc_in, tiles, *rest, drifts):
     if drifts:
-        mine, theirs, accs, tbuf, stage, ext, tsem = rest[-7:]
-        pieces = rest[:-7]
+        mine, theirs, accs, stage, ext = rest[-5:]
+        pieces = rest[:-5]
     else:
-        mine, theirs, accs, tbuf, stage, tsem = rest[-6:]
-        pieces = rest[:-6]
-    late = len(sizes(2))
-    add_pieces(codes, off, tiles, other, pieces[-late:], accs, tbuf, stage, tsem)
+        mine, theirs, accs, stage = rest[-4:]
+        pieces = rest[:-4]
+    accs[:, 0 : 2 * ROWS, :] = jnp.zeros((UNROLL, 2 * ROWS, W), jnp.float32)
+    late = pieces[-len(sizes(2)) :]
+    for p, ref in enumerate(late):
+        fill_stage(codes, off[p], off[p + 1], ref, stage)
+
+    def body(g, c):
+        for u in range(UNROLL):
+            t = g * UNROLL + u
+            accs[u, pl.ds((codes[t] & 7) * TS, TS), :] += jnp.dot(
+                tiles[t], stage[t], preferred_element_type=jnp.float32
+            )
+        return c
+
+    lax.fori_loop(0, groups_of(off[len(late)]), body, 0)
     mine[0:ROWS, :] = acc_in[0:ROWS, :] + total_of(accs, 0, ROWS)
     theirs[0:ROWS, :] = acc_in[ROWS:, :] + total_of(accs, ROWS, ROWS)
     if drifts:
@@ -368,27 +416,36 @@
     )
 
 
-def list_shapes():
-    shapes = []
-    for group in (0, 1, 2):
-        shapes.append(jax.ShapeDtypeStruct((2 * sum(sizes(group)) + 8,), jnp.int32))
-        shapes.append(jax.ShapeDtypeStruct((8,), jnp.int32))
-    return shapes
-
-
-def early(order, skip, pos, pos2, jtab, own, tiles, cached, block):
+def plan(order, skip, pos, pos2, jtab, own):
+    def ints(n):
+        return jax.ShapeDtypeStruct((n,), jnp.int32)
+
+    shapes = [ints(NB + 8), ints(1)]
+    for group in range(3):
+        shapes += [ints(2 * sum(sizes(group)) + 8), ints(8)]
+    lists = pl.pallas_call(
+        plan_kernel,
+        out_shape=tuple(shapes * 2),
+        in_specs=[SMEM] * 6,
+        out_specs=tuple([SMEM] * 16),
+        scratch_shapes=[pltpu.SMEM((NB,), jnp.int32)],
+        compiler_params=params(2),
+        cost_estimate=cost(24),
+        name="plan",
+    )(order, skip, pos, pos2, jtab, own)
+    return lists[:8], lists[8:]
+
+
+def early(own, clist, nc, tiles, cached, block):
     return pl.pallas_call(
         early_kernel,
         out_shape=(
             jax.ShapeDtypeStruct((ROWS, W), jnp.float32),
-            *list_shapes(),
             jax.ShapeDtypeStruct((8, W), jnp.float32),
         ),
-        in_specs=[SMEM] * 6 + [HBM] * 2 + [VMEM],
-        out_specs=(VMEM, *[SMEM] * 6, VMEM),
+        in_specs=[SMEM] * 3 + [HBM] * 2 + [VMEM],
+        out_specs=(VMEM, VMEM),
         scratch_shapes=[
-            pltpu.SMEM((NB + 8,), jnp.int32),
-            pltpu.SMEM((NB,), jnp.int32),
             ACCS,
             *ring_of(32),
             pltpu.VMEM((32, TS, W), jnp.bfloat16),
@@ -400,7 +457,7 @@
         compiler_params=params(16),
         cost_estimate=cost(72),
         name="early_sum",
-    )(order, skip, pos, pos2, jtab, own, tiles, cached, block)
+    )(own, clist, nc, tiles, cached, block)
 
 
 def mid_sum(group, codes, off, acc, tiles, other, pieces):
@@ -416,20 +473,40 @@
     )(codes, off, acc, tiles, other, *pieces)
 
 
-def late_sum(codes, off, jtab, acc, tiles, other, pieces, drifts):
+def mid_fetch(next_codes, next_off, codes, off, acc, tiles, other, pieces):
+    blocks = sum(sizes(1))
+    ahead = 2 * sum(sizes(2)) + UNROLL
+    return pl.pallas_call(
+        mid_fetch_kernel,
+        out_shape=(
+            jax.ShapeDtypeStruct((2 * ROWS, W), jnp.float32),
+            jax.ShapeDtypeStruct((ahead, TS, TS), jnp.bfloat16),
+        ),
+        in_specs=[SMEM] * 4 + [VMEM] + [HBM] * 2 + [VMEM] * len(pieces),
+        out_specs=(VMEM, VMEM),
+        scratch_shapes=[
+            ACCS, *ring_of(32), stage_of(blocks), sems_of(32), sems_of(ahead)
+        ],
+        compiler_params=params(24),
+        cost_estimate=cost(blocks),
+        name="mid1_sum",
+    )(next_codes, next_off, codes, off, acc, tiles, other, *pieces)
+
+
+def late_sum(codes, off, jtab, acc, tiles, pieces, drifts):
     blocks = sum(sizes(2))
     rows = ROWS + 16 if drifts else ROWS
     extra = [pltpu.VMEM((NB, 16, W), jnp.float32)] if drifts else []
     return pl.pallas_call(
         functools.partial(late_kernel, drifts=drifts),
         out_shape=(jax.ShapeDtypeStruct((rows, W), jnp.float32),) * 2,
-        in_specs=[SMEM] * 3 + [VMEM] + [HBM] * 2 + [VMEM] * len(pieces),
+        in_specs=[SMEM] * 3 + [VMEM] * (2 + len(pieces)),
         out_specs=(VMEM, VMEM),
-        scratch_shapes=[ACCS, *ring_of(32), stage_of(blocks), *extra, sems_of(32)],
-        compiler_params=params(20),
+        scratch_shapes=[ACCS, stage_of(blocks), *extra],
+        compiler_params=params(16),
         cost_estimate=cost(blocks),
         name="late_sum",
-    )(codes, off, jtab, acc, tiles, other, *pieces)
+    )(codes, off, jtab, acc, tiles, *pieces)
 
 
 def finish_first(own, mine, theirs, drift, weight, cached):
@@ -464,15 +541,14 @@
     return pltpu.with_memory_space_constraint(value, pltpu.HBM)
 
 
-def layer(block, order, skip, pos, pos2, jtab, own, tiles, other, cached, drifts):
+def layer(block, lists, jtab, own, tiles, other, cached, drifts):
+    clist, nc, list0, off0, list1, off1, list2, off2 = lists
     mid0, mid1, late = gather(block)
-    acc, list1, off1, list2, off2, list3, off3, drift = early(
-        order, skip, pos, pos2, jtab, own, tiles, cached, block
-    )
-    acc = mid_sum(0, list1, off1, acc, tiles, other, mid0)
-    acc = mid_sum(1, list2, off2, acc, tiles, other, mid1)
+    acc, drift = early(own, clist, nc, tiles, cached, block)
+    acc = mid_sum(0, list0, off0, acc, tiles, other, mid0)
+    acc, fetched = mid_fetch(list2, off2, list1, off1, acc, tiles, other, mid1)
     pieces = mid0 + mid1 + late if drifts else late
-    mine, theirs = late_sum(list3, off3, jtab, acc, tiles, other, pieces, drifts)
+    mine, theirs = late_sum(list2, off2, jtab, acc, fetched, pieces, drifts)
     return mine, swap(theirs), drift
 
 
@@ -485,12 +561,13 @@
     pos2 = swap(pos)
     other = in_hbm(swap(tiles[0]))
     tiles = in_hbm(tiles[0])
+    first, second = plan(order.reshape(2 * NB), skip.reshape(2 * NB), pos, pos2, jtab, own)
     mine, theirs, drift = layer(
-        features, order[0], skip[0], pos, pos2, jtab, own, tiles, other, cache_in, False
+        features, first, jtab, own, tiles, other, cache_in, False
     )
     payload = finish_first(own, mine, theirs, drift, w_first, cache_hidden)
     mine, theirs, _ = layer(
-        payload, order[1], skip[1], pos, pos2, jtab, own, tiles, other, cache_hidden, True
+        payload, second, jtab, own, tiles, other, cache_hidden, True
     )
     return finish_second(mine, theirs, w_second)
 

time: 177 us -> 176 us (level)
  starting transfers between devices: 44.4 us -> 56.1 us
  waiting for transfers between devices: 73.8 us -> 62.7 us
  Pallas kernels: 55.3 us -> 49.9 us
  local copies, waits for them, and re-layouts: 1.32 us -> 4.68 us
    pallas_call x0 -> x3, Pallas kernels: none -> 14.5 us  [the longest x2 10.3 us: mid_fetch(): pl.pallas_call(mid_fetch_kernel, out_shape=(jax.ShapeDtypeStruct((2 * ROW...]
    ppermute x30 -> x32, waiting for transfers between devices: 70.4 us -> 60 us  [shift(): return lax.ppermute(value, AXES, PERM[stage, k])]
    pallas_call x4 -> x2, Pallas kernels: 19.8 us -> 9.47 us  [mid_sum(): pl.pallas_call(mid_kernel, out_shape=jax.ShapeDtypeStruct((2 * ROWS, W),...]
    ppermute x30 -> x32, starting transfers between devices: 40.3 us -> 47 us  [shift(): return lax.ppermute(value, AXES, PERM[stage, k])]
    pallas_call x2, Pallas kernels: 24.2 us -> 18.8 us  [early(): pl.pallas_call(early_kernel, out_shape=(jax.ShapeDtypeStruct((ROWS, W), j...]
    ppermute x4, starting transfers between devices: 4.05 us -> 9.12 us  [swap(): return lax.ppermute(value, AXES, SWAP)]
    pallas_call x2, Pallas kernels: 9.45 us -> 5.24 us  [late_sum(): pl.pallas_call(functools.partial(late_kernel, drifts=drifts), out_shape=(...]
  transfers between devices with their start and end apart: 34 -> 36, of which waited for: 17 -> 14; matrix products, arithmetic and copies ran while one was open for 1% -> 2% of each run, Pallas kernels for 25% -> 24%
where the time goes in v2:
time: 176 us
  waiting for transfers between devices  62.7 us (36%)
  starting transfers between devices  56.1 us (32%)
  Pallas kernels  49.9 us (28%)
  local copies, waits for them, and re-layouts  4.68 us (3%)
    ppermute x32, waiting for transfers between devices, shift(): return lax.ppermute(value, AXES, PERM[stage, k])  60 us
    ppermute x32, starting transfers between devices, shift(): return lax.ppermute(value, AXES, PERM[stage, k])  47 us
    pallas_call x2, Pallas kernels, early(): pl.pallas_call(early_kernel, out_shape=(jax.ShapeDtypeStruct((ROWS, W), j...  18.8 us
    pallas_call x2, Pallas kernels, mid_fetch(): pl.pallas_call(mid_fetch_kernel, out_shape=(jax.ShapeDtypeStruct((2 * ROW...  10.3 us
    pallas_call x2, Pallas kernels, mid_sum(): pl.pallas_call(mid_kernel, out_shape=jax.ShapeDtypeStruct((2 * ROWS, W),...  9.47 us
    ppermute x4, starting transfers between devices, swap(): return lax.ppermute(value, AXES, SWAP)  9.12 us
    pallas_call x2, Pallas kernels, late_sum(): pl.pallas_call(functools.partial(late_kernel, drifts=drifts), out_shape=(...  5.24 us
    pallas_call x1, Pallas kernels, plan(): pl.pallas_call(plan_kernel, out_shape=tuple(shapes * 2), in_specs=[SMEM]...  4.23 us
  transfers between devices with their start and end apart: 36, of which 14 were waited for; matrix products, arithmetic and copies ran while one was open for 2% of the time, Pallas kernels for 24%

profile of v2, /device:TPU:1, one launch (start us, length us, event | category | flops | bytes accessed | tf_op | source)
XLA Modules:
  0.0 175.6 jit_solution(7287347149536431175)
XLA Ops:
  3.4 2.5 %collective-permute-start.3 = (bf16[1,512,128]{2,1,0:T(8,128)(2,1)}, bf16[1,512,128]{2,1,0:T(8,128)(2,1)S(1)}, u32[]{:S(2)}, u32[]{:S(2)}) collective-permute-start(bf16[1,512,128]{2,1,0:T(8,128)(2,1)} %bitcast.13), channel_id=1, source_target_pairs={{0,1},{1,0},{2,3},{3,2},{4,5},{5,4},{6,7},{7,6},{8,40},{9,41},{10,... | collective-permute-start | bytes 393224 | tf_op jit(solution)/shard_map/ppermute | solution.py:56
  7.6 2.5 %collective-permute-done.3 = bf16[1,512,128]{2,1,0:T(8,128)(2,1)S(1)} collective-permute-done((bf16[1,512,128]{2,1,0:T(8,128)(2,1)}, bf16[1,512,128]{2,1,0:T(8,128)(2,1)S(1)}, u32[]{:S(2)}, u32[]{:S(2)}) %collective-permute-start.3) | collective-permute-done | bytes 131104 | tf_op jit(solution)/shard_map/ppermute | solution.py:56
  12.9 2.2 %collective-permute-start.9 = (bf16[4,512,128]{2,1,0:T(8,128)(2,1)S(1)}, bf16[4,512,128]{2,1,0:T(8,128)(2,1)S(1)}, u32[]{:S(2)}, u32[]{:S(2)}) collective-permute-start(bf16[4,512,128]{2,1,0:T(8,128)(2,1)S(1)} %pad_maximum_fusion.1.rest_0_), channel_id=1, source_target_pairs={{0,6},{1,7},{2,0},{3,1},{4,2},{5,3},{6,4},{7,5},{8,14},{9,15},{10,... | collective-permute-start | bytes 1572872 | tf_op jit(solution)/shard_map/ppermute | solution.py:56
  15.1 10.5 %collective-permute-done.8 = bf16[4,512,128]{2,1,0:T(8,128)(2,1)S(1)} collective-permute-done((bf16[4,512,128]{2,1,0:T(8,128)(2,1)S(1)}, bf16[4,512,128]{2,1,0:T(8,128)(2,1)S(1)}, u32[]{:S(2)}, u32[]{:S(2)}) %collective-permute-start.8) | collective-permute-done | bytes 524320 | tf_op jit(solution)/shard_map/ppermute | solution.py:56
  29.4 2.4 %collective-permute-start = (s32[256]{0:T(256)S(1)}, s32[256]{0:T(256)S(1)}, u32[]{:S(2)}, u32[]{:S(2)}) collective-permute-start(s32[256]{0:T(256)S(1)} %reshape_squeeze.3.pos), channel_id=1, source_target_pairs={{0,8},{1,9},{2,10},{3,11},{4,12},{5,13},{6,14},{7,15},{8,0},{9,1},... | collective-permute-start | bytes 3080 | tf_op jit(solution)/shard_map/ppermute | solution.py:60
  31.7 2.6 %collective-permute-start.10 = (bf16[4,512,128]{2,1,0:T(8,128)(2,1)}, bf16[4,512,128]{2,1,0:T(8,128)(2,1)}, u32[]{:S(2)}, u32[]{:S(2)}) collective-permute-start(bf16[4,512,128]{2,1,0:T(8,128)(2,1)} %copy-done), channel_id=1, source_target_pairs={{0,4},{1,5},{2,6},{3,7},{4,0},{5,1},{6,2},{7,3},{8,12},{9,13},{10,... | collective-permute-start | bytes 1572872 | tf_op jit(solution)/shard_map/ppermute | solution.py:56
  35.6 11.3 %collective-permute-done.10.rest_5_ = bf16[4,512,128]{2,1,0:T(8,128)(2,1)} collective-permute-done((bf16[4,512,128]{2,1,0:T(8,128)(2,1)}, bf16[4,512,128]{2,1,0:T(8,128)(2,1)}, u32[]{:S(2)}, u32[]{:S(2)}) %collective-permute-start.10) | collective-permute-done | bytes 524320 | tf_op jit(solution)/shard_map/ppermute | solution.py:56
  46.9 2.7 %collective-permute-start.6 = (bf16[4,512,128]{2,1,0:T(8,128)(2,1)}, bf16[4,512,128]{2,1,0:T(8,128)(2,1)S(1)}, u32[]{:S(2)}, u32[]{:S(2)}) collective-permute-start(bf16[4,512,128]{2,1,0:T(8,128)(2,1)} %copy-done), channel_id=1, source_target_pairs={{0,48},{1,49},{2,50},{3,51},{4,52},{5,53},{6,54},{7,55},{8,73},{9,... | collective-permute-start | bytes 1572872 | tf_op jit(solution)/shard_map/ppermute | solution.py:56
  51.5 2.0 %collective-permute-start.14 = (bf16[4,512,128]{2,1,0:T(8,128)(2,1)}, bf16[4,512,128]{2,1,0:T(8,128)(2,1)}, u32[]{:S(2)}, u32[]{:S(2)}) collective-permute-start(bf16[4,512,128]{2,1,0:T(8,128)(2,1)} %collective-permute-done.10.rest_5_), channel_id=1, source_target_pairs={{0,48},{1,49},{2,50},{3,51},{4,52},{5,53},{6,54},{7,55},{8,73},{9,... | collective-permute-start | bytes 1572872 | tf_op jit(solution)/shard_map/ppermute | solution.py:56
  55.2 6.6 %collective-permute-done.6.rest_2_ = bf16[4,512,128]{2,1,0:T(8,128)(2,1)S(1)} collective-permute-done((bf16[4,512,128]{2,1,0:T(8,128)(2,1)}, bf16[4,512,128]{2,1,0:T(8,128)(2,1)S(1)}, u32[]{:S(2)}, u32[]{:S(2)}) %collective-permute-start.6) | collective-permute-done | bytes 524320 | tf_op jit(solution)/shard_map/ppermute | solution.py:56
  63.4 3.4 %collective-permute-start.15 = (bf16[4,512,128]{2,1,0:T(8,128)(2,1)}, bf16[4,512,128]{2,1,0:T(8,128)(2,1)}, u32[]{:S(2)}, u32[]{:S(2)}) collective-permute-start(bf16[4,512,128]{2,1,0:T(8,128)(2,1)} %slice.16), channel_id=1, source_target_pairs={{0,48},{1,49},{2,50},{3,51},{4,52},{5,53},{6,54},{7,55},{8,73},{9,... | collective-permute-start | bytes 1572872 | tf_op jit(solution)/shard_map/ppermute | solution.py:56
  67.4 4.2 %plan.1 = (s32[136]{0:T(256)S(1)}, s32[1]{0:T(128)}, s32[64]{0:T(128)S(1)}, s32[8]{0:T(128)S(1)}, s32[56]{0:T(128)S(1)}, /*index=5*/s32[8]{0:T(128)S(1)}, s32[32...) custom-call(s32[256]{0:T(256)S(1)} %bitcast.16, ...), custom_call_target="tpu_custom_call" | custom-call | flops 402653184 | bytes 4718592 | tf_op jit(solution)/shard_map/plan/pallas_call | solution.py:426
  71.7 9.4 %early_sum.2 = (f32[512,128]{1,0:T(8,128)S(1)}, f32[8,128]{1,0:T(8,128)S(1)}) custom-call(s32[1]{0:T(128)} %bitcast.2.own, s32[136]{0:T(256)S(1)} %get-tuple-element.43.clist, s32[1]{0:T(128)} %get-tuple-element.44.nc, bf16[128,256,256]{2,1,0:T(8,128)(2,1)} %bitcast.19, bf16[128,512,128]{2,1,0:T(8,128)(2,1)} %bitcast.27, bf16[512,128]{1,0:T(8,128)(2,1)S(1)} %copy-done.8), custom_call_target="tpu_custom_call" | custom-call | flops 1207959552 | bytes 14155776 | tf_op jit(solution)/shard_map/early_sum/pallas_call | solution.py:440
  81.1 5.3 %shard_map.131.acc_in = f32[1024,128]{1,0:T(8,128)S(1)} custom-call(s32[64]{0:T(128)S(1)} %get-tuple-element.41.codes, s32[8]{0:T(128)S(1)} %get-tuple-element.42.off, f32[512,128]{1,0:T(8,128)S(1)} %get-tuple-element.45.acc_in, bf16[128,256,256]{2,1,0:T(8,128)(2,1)} %bitcast.20, bf16[128,256,256]{2,1,0:T(8,128)(2,1)} %collective-permute-done.1.other, ...), custom_call_target="tpu_custom_call" | custom-call | flops 469762048 | bytes 5505024 | tf_op jit(solution)/shard_map/pallas_call | solution.py:465
  86.5 5.2 %mid1_sum.2 = (f32[1024,128]{1,0:T(8,128)S(1)}, bf16[28,256,256]{2,1,0:T(8,128)(2,1)S(1)}) custom-call(s32[32]{0:T(128)S(1)} %get-tuple-element.37.next_codes.codes, s32[8]{0:T(128)S(1)} %get-tuple-element.38.next_off.off, s32[56]{0:T(128)S(1)} %get-tuple-element.39.codes, s32[8]{0:T(128)S(1)} %get-tuple-element.40.off, f32[1024,128]{1,0:T(8,128)S(1)} %shard_map.131.acc_in, ...), custom_call_target="tpu_custom_call" | custom-call | flops 402653184 | bytes 4718592 | tf_op jit(solution)/shard_map/mid1_sum/pallas_call | solution.py:479
  91.7 3.2 %late_sum.2 = (f32[512,128]{1,0:T(8,128)S(1)}, f32[512,128]{1,0:T(8,128)S(1)}) custom-call(s32[32]{0:T(128)S(1)} %get-tuple-element.37.next_codes.codes, s32[8]{0:T(128)S(1)} %get-tuple-element.38.next_off.off, s32[64]{0:T(128)S(1)} %fusion.8.jtab, f32[1024,128]{1,0:T(8,128)S(1)} %get-tuple-element.46.acc_in, ...), custom_call_target="tpu_custom_call" | custom-call | flops 201326592 | bytes 2359296 | tf_op jit(solution)/shard_map/late_sum/pallas_call | solution.py:500
  97.6 2.3 %collective-permute-start.20 = (bf16[1,528,128]{2,1,0:T(8,128)(2,1)S(1)}, bf16[1,528,128]{2,1,0:T(8,128)(2,1)S(1)}, u32[]{:S(2)}, u32[]{:S(2)}) collective-permute-start(bf16[1,528,128]{2,1,0:T(8,128)(2,1)S(1)} %bitcast.9), channel_id=1, source_target_pairs={{0,1},{1,0},{2,3},{3,2},{4,5},{5,4},{6,7},{7,6},{8,40},{9,41},{10,... | collective-permute-start | bytes 405512 | tf_op jit(solution)/shard_map/ppermute | solution.py:56
  100.3 4.0 %collective-permute-done.19 = bf16[1,528,128]{2,1,0:T(8,128)(2,1)S(1)} collective-permute-done((bf16[1,528,128]{2,1,0:T(8,128)(2,1)S(1)}, bf16[1,528,128]{2,1,0:T(8,128)(2,1)S(1)}, u32[]{:S(2)}, u32[]{:S(2)}) %collective-permute-start.19) | collective-permute-done | bytes 135200 | tf_op jit(solution)/shard_map/ppermute | solution.py:56
  107.9 10.8 %collective-permute-done.25 = bf16[4,528,128]{2,1,0:T(8,128)(2,1)S(1)} collective-permute-done((bf16[4,528,128]{2,1,0:T(8,128)(2,1)S(1)}, bf16[4,528,128]{2,1,0:T(8,128)(2,1)S(1)}, u32[]{:S(2)}, u32[]{:S(2)}) %collective-permute-start.25) | collective-permute-done | bytes 540704 | tf_op jit(solution)/shard_map/ppermute | solution.py:56
  118.9 2.1 %collective-permute-start.28 = (bf16[8,528,128]{2,1,0:T(8,128)(2,1)S(1)}, bf16[8,528,128]{2,1,0:T(8,128)(2,1)S(1)}, u32[]{:S(2)}, u32[]{:S(2)}) collective-permute-start(bf16[8,528,128]{2,1,0:T(8,128)(2,1)S(1)} %constant_dynamic-update-slice_fusion.2.rest_4_), channel_id=1, source_target_pairs={{0,16},{1,17},{2,18},{3,19},{4,20},{5,21},{6,22},{7,23},{8,72},{9,... | collective-permute-start | bytes 3244040 | tf_op jit(solution)/shard_map/ppermute | solution.py:56
  121.6 2.5 %collective-permute-start.27 = (bf16[4,528,128]{2,1,0:T(8,128)(2,1)S(1)}, bf16[4,528,128]{2,1,0:T(8,128)(2,1)S(1)}, u32[]{:S(2)}, u32[]{:S(2)}) collective-permute-start(bf16[4,528,128]{2,1,0:T(8,128)(2,1)S(1)} %pad_maximum_fusion.rest_0_), channel_id=1, source_target_pairs={{0,4},{1,5},{2,6},{3,7},{4,0},{5,1},{6,2},{7,3},{8,12},{9,13},{10,... | collective-permute-start | bytes 1622024 | tf_op jit(solution)/shard_map/ppermute | solution.py:56
  124.2 2.7 %collective-permute-start.23 = (bf16[4,528,128]{2,1,0:T(8,128)(2,1)S(1)}, bf16[4,528,128]{2,1,0:T(8,128)(2,1)S(1)}, u32[]{:S(2)}, u32[]{:S(2)}) collective-permute-start(bf16[4,528,128]{2,1,0:T(8,128)(2,1)S(1)} %pad_maximum_fusion.rest_0_), channel_id=1, source_target_pairs={{0,48},{1,49},{2,50},{3,51},{4,52},{5,53},{6,54},{7,55},{8,73},{9,... | collective-permute-start | bytes 1622024 | tf_op jit(solution)/shard_map/ppermute | solution.py:56
  126.9 7.2 %collective-permute-done.27.rest_5_ = bf16[4,528,128]{2,1,0:T(8,128)(2,1)S(1)} collective-permute-done((bf16[4,528,128]{2,1,0:T(8,128)(2,1)S(1)}, bf16[4,528,128]{2,1,0:T(8,128)(2,1)S(1)}, u32[]{:S(2)}, u32[]{:S(2)}) %collective-permute-start.27) | collective-permute-done | bytes 540704 | tf_op jit(solution)/shard_map/ppermute | solution.py:56
  135.3 2.2 %collective-permute-start.31 = (bf16[4,528,128]{2,1,0:T(8,128)(2,1)S(1)}, bf16[4,528,128]{2,1,0:T(8,128)(2,1)S(1)}, u32[]{:S(2)}, u32[]{:S(2)}) collective-permute-start(bf16[4,528,128]{2,1,0:T(8,128)(2,1)S(1)} %collective-permute-done.27.rest_5_), channel_id=1, source_target_pairs={{0,48},{1,49},{2,50},{3,51},{4,52},{5,53},{6,54},{7,55},{8,73},{9,... | collective-permute-start | bytes 1622024 | tf_op jit(solution)/shard_map/ppermute | solution.py:56
  137.6 2.7 %collective-permute-done.22.rest_1_ = bf16[4,528,128]{2,1,0:T(8,128)(2,1)S(1)} collective-permute-done((bf16[4,528,128]{2,1,0:T(8,128)(2,1)S(1)}, bf16[4,528,128]{2,1,0:T(8,128)(2,1)S(1)}, u32[]{:S(2)}, u32[]{:S(2)}) %collective-permute-start.22) | collective-permute-done | bytes 540704 | tf_op jit(solution)/shard_map/ppermute | solution.py:56
  141.4 2.1 %collective-permute-start.32 = (bf16[4,528,128]{2,1,0:T(8,128)(2,1)S(1)}, bf16[4,528,128]{2,1,0:T(8,128)(2,1)S(1)}, u32[]{:S(2)}, u32[]{:S(2)}) collective-permute-start(bf16[4,528,128]{2,1,0:T(8,128)(2,1)S(1)} %slice.18), channel_id=1, source_target_pairs={{0,48},{1,49},{2,50},{3,51},{4,52},{5,53},{6,54},{7,55},{8,73},{9,... | collective-permute-start | bytes 1622024 | tf_op jit(solution)/shard_map/ppermute | solution.py:56
  143.5 3.0 %collective-permute-done.24.rest_3_ = bf16[4,528,128]{2,1,0:T(8,128)(2,1)S(1)} collective-permute-done((bf16[4,528,128]{2,1,0:T(8,128)(2,1)S(1)}, bf16[4,528,128]{2,1,0:T(8,128)(2,1)S(1)}, u32[]{:S(2)}, u32[]{:S(2)}) %collective-permute-start.24) | collective-permute-done | bytes 540704 | tf_op jit(solution)/shard_map/ppermute | solution.py:56
  147.4 9.4 %early_sum.3 = (f32[512,128]{1,0:T(8,128)S(1)}, f32[8,128]{1,0:T(8,128)}) custom-call(s32[1]{0:T(128)} %bitcast.2.own, s32[136]{0:T(256)S(1)} %get-tuple-element.35.clist, s32[1]{0:T(128)} %get-tuple-element.36.nc, bf16[128,256,256]{2,1,0:T(8,128)(2,1)} %bitcast.22, bf16[128,512,128]{2,1,0:T(8,128)(2,1)} %bitcast.26, bf16[528,128]{1,0:T(8,128)(2,1)S(1)} %finish_first.1.block), custom_call_target="tpu_custom_call" | custom-call | flops 1207959552 | bytes 14155776 | tf_op jit(solution)/shard_map/early_sum/pallas_call | solution.py:440
  156.8 4.1 %shard_map.132.acc_in = f32[1024,128]{1,0:T(8,128)S(1)} custom-call(s32[64]{0:T(128)S(1)} %get-tuple-element.33.codes, s32[8]{0:T(128)S(1)} %get-tuple-element.34.off, f32[512,128]{1,0:T(8,128)S(1)} %get-tuple-element.51.acc_in, bf16[128,256,256]{2,1,0:T(8,128)(2,1)} %bitcast.23, bf16[128,256,256]{2,1,0:T(8,128)(2,1)} %collective-permute-done.1.other, ...), custom_call_target="tpu_custom_call" | custom-call | flops 469762048 | bytes 5505024 | tf_op jit(solution)/shard_map/pallas_call | solution.py:465
  161.0 5.2 %mid1_sum.3 = (f32[1024,128]{1,0:T(8,128)S(1)}, bf16[28,256,256]{2,1,0:T(8,128)(2,1)S(1)}) custom-call(s32[32]{0:T(128)S(1)} %get-tuple-element.29.next_codes.codes, s32[8]{0:T(128)S(1)} %get-tuple-element.30.next_off.off, s32[56]{0:T(128)S(1)} %get-tuple-element.31.codes, s32[8]{0:T(128)S(1)} %get-tuple-element.32.off, f32[1024,128]{1,0:T(8,128)S(1)} %shard_map.132.acc_in, ...), custom_call_target="tpu_custom_call" | custom-call | flops 402653184 | bytes 4718592 | tf_op jit(solution)/shard_map/mid1_sum/pallas_call | solution.py:479
  166.2 2.1 %late_sum.3 = (f32[528,128]{1,0:T(8,128)S(1)}, f32[528,128]{1,0:T(8,128)S(1)}) custom-call(s32[32]{0:T(128)S(1)} %get-tuple-element.29.next_codes.codes, s32[8]{0:T(128)S(1)} %get-tuple-element.30.next_off.off, s32[64]{0:T(128)S(1)} %fusion.8.jtab, f32[1024,128]{1,0:T(8,128)S(1)} %get-tuple-element.52.acc_in, ...), custom_call_target="tpu_custom_call" | custom-call | flops 201326592 | bytes 2359296 | tf_op jit(solution)/shard_map/late_sum/pallas_call | solution.py:500
  168.3 5.2 %collective-permute-start.35 = (f32[528,128]{1,0:T(8,128)S(1)}, f32[528,128]{1,0:T(8,128)S(1)}, u32[]{:S(2)}, u32[]{:S(2)}) collective-permute-start(f32[528,128]{1,0:T(8,128)S(1)} %get-tuple-element.55), channel_id=1, source_target_pairs={{0,8},{1,9},{2,10},{3,11},{4,12},{5,13},{6,14},{7,15},{8,0},{9,1},... | collective-permute-start | bytes 811016 | tf_op jit(solution)/shard_map/ppermute | solution.py:60
  (98 shorter events, 30.8 us)
Async XLA Ops:
  0.6 66.1 %collective-permute-start.1 = (bf16[128,256,256]{2,1,0:T(8,128)(2,1)}, bf16[128,256,256]{2,1,0:T(8,128)(2,1)}, u32[]{:S(2)}, u32[]{:S(2)}) collective-permute-start(bf16[128,256,256]{2,1,0:T(8,128)(2,1)} %bitcast.18), channel_id=1, source_target_pairs={{0,8},{1,9},{2,10},{3,11},{4,12},{5,13},{6,14},{7,15},{8,0},{9,1},... | collective-permute-start | bytes 50331656 | tf_op jit(solution)/shard_map/ppermute | solution.py:60
  2.1 5.5 %collective-permute-start.2 = (bf16[1,512,128]{2,1,0:T(8,128)(2,1)}, bf16[1,512,128]{2,1,0:T(8,128)(2,1)S(1)}, u32[]{:S(2)}, u32[]{:S(2)}) collective-permute-start(bf16[1,512,128]{2,1,0:T(8,128)(2,1)} %bitcast.12), channel_id=1, source_target_pairs={{0,64},{1,65},{2,66},{3,67},{4,68},{5,69},{6,70},{7,71},{8,24},{9,... | collective-permute-start | bytes 393224 | tf_op jit(solution)/shard_map/ppermute | solution.py:56
  3.4 6.7 %collective-permute-start.3 = (bf16[1,512,128]{2,1,0:T(8,128)(2,1)}, bf16[1,512,128]{2,1,0:T(8,128)(2,1)S(1)}, u32[]{:S(2)}, u32[]{:S(2)}) collective-permute-start(bf16[1,512,128]{2,1,0:T(8,128)(2,1)} %bitcast.13), channel_id=1, source_target_pairs={{0,1},{1,0},{2,3},{3,2},{4,5},{5,4},{6,7},{7,6},{8,40},{9,41},{10,... | collective-permute-start | bytes 393224 | tf_op jit(solution)/shard_map/ppermute | solution.py:56
  11.2 14.4 %collective-permute-start.8 = (bf16[4,512,128]{2,1,0:T(8,128)(2,1)S(1)}, bf16[4,512,128]{2,1,0:T(8,128)(2,1)S(1)}, u32[]{:S(2)}, u32[]{:S(2)}) collective-permute-start(bf16[4,512,128]{2,1,0:T(8,128)(2,1)S(1)} %pad_maximum_fusion.1.rest_0_), channel_id=1, source_target_pairs={{0,2},{1,3},{2,4},{3,5},{4,6},{5,7},{6,0},{7,1},{8,10},{9,11},{10,... | collective-permute-start | bytes 1572872 | tf_op jit(solution)/shard_map/ppermute | solution.py:56
  12.9 12.7 %collective-permute-start.9 = (bf16[4,512,128]{2,1,0:T(8,128)(2,1)S(1)}, bf16[4,512,128]{2,1,0:T(8,128)(2,1)S(1)}, u32[]{:S(2)}, u32[]{:S(2)}) collective-permute-start(bf16[4,512,128]{2,1,0:T(8,128)(2,1)S(1)} %pad_maximum_fusion.1.rest_0_), channel_id=1, source_target_pairs={{0,6},{1,7},{2,0},{3,1},{4,2},{5,3},{6,4},{7,5},{8,14},{9,15},{10,... | collective-permute-start | bytes 1572872 | tf_op jit(solution)/shard_map/ppermute | solution.py:56
  25.7 25.1 %collective-permute-start.11 = (bf16[8,512,128]{2,1,0:T(8,128)(2,1)S(1)}, bf16[8,512,128]{2,1,0:T(8,128)(2,1)S(1)}, u32[]{:S(2)}, u32[]{:S(2)}) collective-permute-start(bf16[8,512,128]{2,1,0:T(8,128)(2,1)S(1)} %constant_dynamic-update-slice_fusion.rest_4_), channel_id=1, source_target_pairs={{0,16},{1,17},{2,18},{3,19},{4,20},{5,21},{6,22},{7,23},{8,72},{9,... | collective-permute-start | bytes 3145736 | tf_op jit(solution)/shard_map/ppermute | solution.py:56
  27.6 23.9 %collective-permute-start.12 = (bf16[8,512,128]{2,1,0:T(8,128)(2,1)S(1)}, bf16[8,512,128]{2,1,0:T(8,128)(2,1)S(1)}, u32[]{:S(2)}, u32[]{:S(2)}) collective-permute-start(bf16[8,512,128]{2,1,0:T(8,128)(2,1)S(1)} %constant_dynamic-update-slice_fusion.rest_4_), channel_id=1, source_target_pairs={{0,48},{1,49},{2,50},{3,51},{4,52},{5,53},{6,54},{7,55},{8,73},{9,... | collective-permute-start | bytes 3145736 | tf_op jit(solution)/shard_map/ppermute | solution.py:56
  31.7 15.2 %collective-permute-start.10 = (bf16[4,512,128]{2,1,0:T(8,128)(2,1)}, bf16[4,512,128]{2,1,0:T(8,128)(2,1)}, u32[]{:S(2)}, u32[]{:S(2)}) collective-permute-start(bf16[4,512,128]{2,1,0:T(8,128)(2,1)} %copy-done), channel_id=1, source_target_pairs={{0,4},{1,5},{2,6},{3,7},{4,0},{5,1},{6,2},{7,3},{8,12},{9,13},{10,... | collective-permute-start | bytes 1572872 | tf_op jit(solution)/shard_map/ppermute | solution.py:56
  34.3 15.4 %collective-permute-start.5 = (bf16[4,512,128]{2,1,0:T(8,128)(2,1)}, bf16[4,512,128]{2,1,0:T(8,128)(2,1)S(1)}, u32[]{:S(2)}, u32[]{:S(2)}) collective-permute-start(bf16[4,512,128]{2,1,0:T(8,128)(2,1)} %copy-done), channel_id=1, source_target_pairs={{0,16},{1,17},{2,18},{3,19},{4,20},{5,21},{6,22},{7,23},{8,72},{9,... | collective-permute-start | bytes 1572872 | tf_op jit(solution)/shard_map/ppermute | solution.py:56
  46.9 14.8 %collective-permute-start.6 = (bf16[4,512,128]{2,1,0:T(8,128)(2,1)}, bf16[4,512,128]{2,1,0:T(8,128)(2,1)S(1)}, u32[]{:S(2)}, u32[]{:S(2)}) collective-permute-start(bf16[4,512,128]{2,1,0:T(8,128)(2,1)} %copy-done), channel_id=1, source_target_pairs={{0,48},{1,49},{2,50},{3,51},{4,52},{5,53},{6,54},{7,55},{8,73},{9,... | collective-permute-start | bytes 1572872 | tf_op jit(solution)/shard_map/ppermute | solution.py:56
  50.5 12.1 %collective-permute-start.7 = (bf16[4,512,128]{2,1,0:T(8,128)(2,1)}, bf16[4,512,128]{2,1,0:T(8,128)(2,1)S(1)}, u32[]{:S(2)}, u32[]{:S(2)}) collective-permute-start(bf16[4,512,128]{2,1,0:T(8,128)(2,1)} %copy-done), channel_id=1, source_target_pairs={{0,32},{1,33},{2,34},{3,35},{4,36},{5,37},{6,38},{7,39},{8,9},{9,8... | collective-permute-start | bytes 1572872 | tf_op jit(solution)/shard_map/ppermute | solution.py:56
  50.8 35.6 %collective-permute-start.13 = (bf16[4,512,128]{2,1,0:T(8,128)(2,1)}, bf16[4,512,128]{2,1,0:T(8,128)(2,1)}, u32[]{:S(2)}, u32[]{:S(2)}) collective-permute-start(bf16[4,512,128]{2,1,0:T(8,128)(2,1)} %collective-permute-done.10.rest_5_), channel_id=1, source_target_pairs={{0,16},{1,17},{2,18},{3,19},{4,20},{5,21},{6,22},{7,23},{8,72},{9,... | collective-permute-start | bytes 1572872 | tf_op jit(solution)/shard_map/ppermute | solution.py:56
  51.5 35.0 %collective-permute-start.14 = (bf16[4,512,128]{2,1,0:T(8,128)(2,1)}, bf16[4,512,128]{2,1,0:T(8,128)(2,1)}, u32[]{:S(2)}, u32[]{:S(2)}) collective-permute-start(bf16[4,512,128]{2,1,0:T(8,128)(2,1)} %collective-permute-done.10.rest_5_), channel_id=1, source_target_pairs={{0,48},{1,49},{2,50},{3,51},{4,52},{5,53},{6,54},{7,55},{8,73},{9,... | collective-permute-start | bytes 1572872 | tf_op jit(solution)/shard_map/ppermute | solution.py:56
  62.5 29.1 %collective-permute-start.17 = (bf16[4,512,128]{2,1,0:T(8,128)(2,1)}, bf16[4,512,128]{2,1,0:T(8,128)(2,1)}, u32[]{:S(2)}, u32[]{:S(2)}) collective-permute-start(bf16[4,512,128]{2,1,0:T(8,128)(2,1)} %collective-permute-done.10.rest_5_), channel_id=1, source_target_pairs={{0,32},{1,33},{2,34},{3,35},{4,36},{5,37},{6,38},{7,39},{8,9},{9,8... | collective-permute-start | bytes 1572872 | tf_op jit(solution)/shard_map/ppermute | solution.py:56
  63.4 28.3 %collective-permute-start.15 = (bf16[4,512,128]{2,1,0:T(8,128)(2,1)}, bf16[4,512,128]{2,1,0:T(8,128)(2,1)}, u32[]{:S(2)}, u32[]{:S(2)}) collective-permute-start(bf16[4,512,128]{2,1,0:T(8,128)(2,1)} %slice.16), channel_id=1, source_target_pairs={{0,48},{1,49},{2,50},{3,51},{4,52},{5,53},{6,54},{7,55},{8,73},{9,... | collective-permute-start | bytes 1572872 | tf_op jit(solution)/shard_map/ppermute | solution.py:56
  66.8 24.9 %collective-permute-start.16 = (bf16[4,512,128]{2,1,0:T(8,128)(2,1)}, bf16[4,512,128]{2,1,0:T(8,128)(2,1)}, u32[]{:S(2)}, u32[]{:S(2)}) collective-permute-start(bf16[4,512,128]{2,1,0:T(8,128)(2,1)} %slice.17), channel_id=1, source_target_pairs={{0,16},{1,17},{2,18},{3,19},{4,20},{5,21},{6,22},{7,23},{8,72},{9,... | collective-permute-start | bytes 1572872 | tf_op jit(solution)/shard_map/ppermute | solution.py:56
  97.5 6.9 %collective-permute-start.19 = (bf16[1,528,128]{2,1,0:T(8,128)(2,1)S(1)}, bf16[1,528,128]{2,1,0:T(8,128)(2,1)S(1)}, u32[]{:S(2)}, u32[]{:S(2)}) collective-permute-start(bf16[1,528,128]{2,1,0:T(8,128)(2,1)S(1)} %bitcast.8), channel_id=1, source_target_pairs={{0,64},{1,65},{2,66},{3,67},{4,68},{5,69},{6,70},{7,71},{8,24},{9,... | collective-permute-start | bytes 405512 | tf_op jit(solution)/shard_map/ppermute | solution.py:56
  97.6 6.8 %collective-permute-start.20 = (bf16[1,528,128]{2,1,0:T(8,128)(2,1)S(1)}, bf16[1,528,128]{2,1,0:T(8,128)(2,1)S(1)}, u32[]{:S(2)}, u32[]{:S(2)}) collective-permute-start(bf16[1,528,128]{2,1,0:T(8,128)(2,1)S(1)} %bitcast.9), channel_id=1, source_target_pairs={{0,1},{1,0},{2,3},{3,2},{4,5},{5,4},{6,7},{7,6},{8,40},{9,41},{10,... | collective-permute-start | bytes 405512 | tf_op jit(solution)/shard_map/ppermute | solution.py:56
  105.1 13.7 %collective-permute-start.25 = (bf16[4,528,128]{2,1,0:T(8,128)(2,1)S(1)}, bf16[4,528,128]{2,1,0:T(8,128)(2,1)S(1)}, u32[]{:S(2)}, u32[]{:S(2)}) collective-permute-start(bf16[4,528,128]{2,1,0:T(8,128)(2,1)S(1)} %pad_maximum_fusion.rest_0_), channel_id=1, source_target_pairs={{0,2},{1,3},{2,4},{3,5},{4,6},{5,7},{6,0},{7,1},{8,10},{9,11},{10,... | collective-permute-start | bytes 1622024 | tf_op jit(solution)/shard_map/ppermute | solution.py:56
  106.1 12.7 %collective-permute-start.26 = (bf16[4,528,128]{2,1,0:T(8,128)(2,1)S(1)}, bf16[4,528,128]{2,1,0:T(8,128)(2,1)S(1)}, u32[]{:S(2)}, u32[]{:S(2)}) collective-permute-start(bf16[4,528,128]{2,1,0:T(8,128)(2,1)S(1)} %pad_maximum_fusion.rest_0_), channel_id=1, source_target_pairs={{0,6},{1,7},{2,0},{3,1},{4,2},{5,3},{6,4},{7,5},{8,14},{9,15},{10,... | collective-permute-start | bytes 1622024 | tf_op jit(solution)/shard_map/ppermute | solution.py:56
  118.9 15.9 %collective-permute-start.28 = (bf16[8,528,128]{2,1,0:T(8,128)(2,1)S(1)}, bf16[8,528,128]{2,1,0:T(8,128)(2,1)S(1)}, u32[]{:S(2)}, u32[]{:S(2)}) collective-permute-start(bf16[8,528,128]{2,1,0:T(8,128)(2,1)S(1)} %constant_dynamic-update-slice_fusion.2.rest_4_), channel_id=1, source_target_pairs={{0,16},{1,17},{2,18},{3,19},{4,20},{5,21},{6,22},{7,23},{8,72},{9,... | collective-permute-start | bytes 3244040 | tf_op jit(solution)/shard_map/ppermute | solution.py:56
  121.0 14.3 %collective-permute-start.29 = (bf16[8,528,128]{2,1,0:T(8,128)(2,1)S(1)}, bf16[8,528,128]{2,1,0:T(8,128)(2,1)S(1)}, u32[]{:S(2)}, u32[]{:S(2)}) collective-permute-start(bf16[8,528,128]{2,1,0:T(8,128)(2,1)S(1)} %constant_dynamic-update-slice_fusion.2.rest_4_), channel_id=1, source_target_pairs={{0,48},{1,49},{2,50},{3,51},{4,52},{5,53},{6,54},{7,55},{8,73},{9,... | collective-permute-start | bytes 3244040 | tf_op jit(solution)/shard_map/ppermute | solution.py:56
  121.6 12.5 %collective-permute-start.27 = (bf16[4,528,128]{2,1,0:T(8,128)(2,1)S(1)}, bf16[4,528,128]{2,1,0:T(8,128)(2,1)S(1)}, u32[]{:S(2)}, u32[]{:S(2)}) collective-permute-start(bf16[4,528,128]{2,1,0:T(8,128)(2,1)S(1)} %pad_maximum_fusion.rest_0_), channel_id=1, source_target_pairs={{0,4},{1,5},{2,6},{3,7},{4,0},{5,1},{6,2},{7,3},{8,12},{9,13},{10,... | collective-permute-start | bytes 1622024 | tf_op jit(solution)/shard_map/ppermute | solution.py:56
  124.2 16.1 %collective-permute-start.22 = (bf16[4,528,128]{2,1,0:T(8,128)(2,1)S(1)}, bf16[4,528,128]{2,1,0:T(8,128)(2,1)S(1)}, u32[]{:S(2)}, u32[]{:S(2)}) collective-permute-start(bf16[4,528,128]{2,1,0:T(8,128)(2,1)S(1)} %pad_maximum_fusion.rest_0_), channel_id=1, source_target_pairs={{0,16},{1,17},{2,18},{3,19},{4,20},{5,21},{6,22},{7,23},{8,72},{9,... | collective-permute-start | bytes 1622024 | tf_op jit(solution)/shard_map/ppermute | solution.py:56
  124.2 17.2 %collective-permute-start.23 = (bf16[4,528,128]{2,1,0:T(8,128)(2,1)S(1)}, bf16[4,528,128]{2,1,0:T(8,128)(2,1)S(1)}, u32[]{:S(2)}, u32[]{:S(2)}) collective-permute-start(bf16[4,528,128]{2,1,0:T(8,128)(2,1)S(1)} %pad_maximum_fusion.rest_0_), channel_id=1, source_target_pairs={{0,48},{1,49},{2,50},{3,51},{4,52},{5,53},{6,54},{7,55},{8,73},{9,... | collective-permute-start | bytes 1622024 | tf_op jit(solution)/shard_map/ppermute | solution.py:56
  134.1 12.4 %collective-permute-start.24 = (bf16[4,528,128]{2,1,0:T(8,128)(2,1)S(1)}, bf16[4,528,128]{2,1,0:T(8,128)(2,1)S(1)}, u32[]{:S(2)}, u32[]{:S(2)}) collective-permute-start(bf16[4,528,128]{2,1,0:T(8,128)(2,1)S(1)} %pad_maximum_fusion.rest_0_), channel_id=1, source_target_pairs={{0,32},{1,33},{2,34},{3,35},{4,36},{5,37},{6,38},{7,39},{8,9},{9,8... | collective-permute-start | bytes 1622024 | tf_op jit(solution)/shard_map/ppermute | solution.py:56
  134.8 26.1 %collective-permute-start.30 = (bf16[4,528,128]{2,1,0:T(8,128)(2,1)S(1)}, bf16[4,528,128]{2,1,0:T(8,128)(2,1)S(1)}, u32[]{:S(2)}, u32[]{:S(2)}) collective-permute-start(bf16[4,528,128]{2,1,0:T(8,128)(2,1)S(1)} %collective-permute-done.27.rest_5_), channel_id=1, source_target_pairs={{0,16},{1,17},{2,18},{3,19},{4,20},{5,21},{6,22},{7,23},{8,72},{9,... | collective-permute-start | bytes 1622024 | tf_op jit(solution)/shard_map/ppermute | solution.py:56
  135.3 25.6 %collective-permute-start.31 = (bf16[4,528,128]{2,1,0:T(8,128)(2,1)S(1)}, bf16[4,528,128]{2,1,0:T(8,128)(2,1)S(1)}, u32[]{:S(2)}, u32[]{:S(2)}) collective-permute-start(bf16[4,528,128]{2,1,0:T(8,128)(2,1)S(1)} %collective-permute-done.27.rest_5_), channel_id=1, source_target_pairs={{0,48},{1,49},{2,50},{3,51},{4,52},{5,53},{6,54},{7,55},{8,73},{9,... | collective-permute-start | bytes 1622024 | tf_op jit(solution)/shard_map/ppermute | solution.py:56
  140.3 25.9 %collective-permute-start.34 = (bf16[4,528,128]{2,1,0:T(8,128)(2,1)S(1)}, bf16[4,528,128]{2,1,0:T(8,128)(2,1)S(1)}, u32[]{:S(2)}, u32[]{:S(2)}) collective-permute-start(bf16[4,528,128]{2,1,0:T(8,128)(2,1)S(1)} %collective-permute-done.27.rest_5_), channel_id=1, source_target_pairs={{0,32},{1,33},{2,34},{3,35},{4,36},{5,37},{6,38},{7,39},{8,9},{9,8... | collective-permute-start | bytes 1622024 | tf_op jit(solution)/shard_map/ppermute | solution.py:56
  141.4 24.7 %collective-permute-start.32 = (bf16[4,528,128]{2,1,0:T(8,128)(2,1)S(1)}, bf16[4,528,128]{2,1,0:T(8,128)(2,1)S(1)}, u32[]{:S(2)}, u32[]{:S(2)}) collective-permute-start(bf16[4,528,128]{2,1,0:T(8,128)(2,1)S(1)} %slice.18), channel_id=1, source_target_pairs={{0,48},{1,49},{2,50},{3,51},{4,52},{5,53},{6,54},{7,55},{8,73},{9,... | collective-permute-start | bytes 1622024 | tf_op jit(solution)/shard_map/ppermute | solution.py:56
  146.5 19.6 %collective-permute-start.33 = (bf16[4,528,128]{2,1,0:T(8,128)(2,1)S(1)}, bf16[4,528,128]{2,1,0:T(8,128)(2,1)S(1)}, u32[]{:S(2)}, u32[]{:S(2)}) collective-permute-start(bf16[4,528,128]{2,1,0:T(8,128)(2,1)S(1)} %slice.19), channel_id=1, source_target_pairs={{0,16},{1,17},{2,18},{3,19},{4,20},{5,21},{6,22},{7,23},{8,72},{9,... | collective-permute-start | bytes 1622024 | tf_op jit(solution)/shard_map/ppermute | solution.py:56
  168.3 6.4 %collective-permute-start.35 = (f32[528,128]{1,0:T(8,128)S(1)}, f32[528,128]{1,0:T(8,128)S(1)}, u32[]{:S(2)}, u32[]{:S(2)}) collective-permute-start(f32[528,128]{1,0:T(8,128)S(1)} %get-tuple-element.55), channel_id=1, source_target_pairs={{0,8},{1,9},{2,10},{3,11},{4,12},{5,13},{6,14},{7,15},{8,0},{9,1},... | collective-permute-start | bytes 811016 | tf_op jit(solution)/shard_map/ppermute | solution.py:60
  (21 other events, 309.4 us)
